TPU v7x, 32 devices: a whole 2x2x4 slice. The times are simulated.
32 devices in a mesh: dp: 8 (over z, x), fsdp: 4 (over y, core).
Axes of the slice: x: 2, y: 2, z: 4, core: 2. Of those that a mesh axis runs over, the one named last changes fastest.
Arguments:
- hidden: bfloat16 [16, 256, 5120], P('dp', None, 'fsdp'), may hold values from -8 to 8
- gain: bfloat16 [5120], P('fsdp'), may hold values from 0.25 to 1.75
- head: bfloat16 [2048, 5120], P('fsdp'), may hold values from -1 to 1
- targets: int32 [16, 256], P('dp'), may hold values from 0 to 2047, as said below
- lengths: int32 [16], P('dp'), may hold values from 1 to 256, 2048 in all
- old_logp: float32 [16, 256], P('dp'), may hold values from -64 to 0
- rewards: float32 [16], P('dp'), may hold values from -6 to 6
- group_slot: int32 [16], P('dp'), may hold values from 0 to 15, each once
Outputs:
- loss: float32 [], replicated
- grad_hidden: bfloat16 [16, 256, 5120], P('dp', None, 'fsdp')
- grad_gain: float32 [5120], P('fsdp')
- grad_head_t: float32 [5120, 2048], P('dp', 'fsdp')
Inputs may be any that keep to these rules, and one draw needn't show every extreme that they name: `lengths`: they sum to 2048 and one of them equals 256. `group_slot`: each value once; responses with equal group_slot // 8 answer one prompt. At position 0, different responses have different targets.
All inputs are finite; a program needn't handle non-finite values. No bound on the sum of `lengths` on one device may be relied on, other than what follows from the above.
Results may differ from a plain program's by a relative error of at most 0.018.
Values may be sent and summed in bfloat16 or wider, within the bound.
A program may use at most 64 MiB of HBM per device.

v0:
```python
import functools
import jax
import jax.numpy as jnp
from jax import lax
from jax.experimental import pallas as pl
from jax.experimental.pallas import tpu as pltpu
from jax.sharding import PartitionSpec as P

GROUP = 8


eps_norm = 1e-06
clip_low = 0.8
clip_high = 1.2
dual_bound = 3.0


MESH = pl.DeviceIdType.MESH


def tail_kernel(
    n_dp,
    n_fsdp,
    feats,
    normed_ref,
    dlogits_ref,
    head_ref,
    hidden_ref,
    gain_ref,
    inv_ref,
    loss_ref,
    gh_ref,
    gw_ref,
    gg_ref,
    x_out,
    x_in,
    n_out,
    n_in,
    z_out,
    z_in,
    c_out,
    c_in,
    y_out,
    y_in,
    acc,
    d_out,
    d_in,
    g_out,
    g_in,
    xs,
    xr,
    ns,
    nr,
    zs,
    zr,
    cs,
    cr,
    ys,
    yr,
    ds_,
    dr,
    gs,
    gr,
):
    dp = lax.axis_index("dp")
    fs = lax.axis_index("fsdp")
    z, x = dp // 2, dp % 2
    y, c = fs // 2, fs % 2
    outer_dp, outer_fs, quads = n_dp // 2, n_fsdp // 2, n_dp // 4
    cols = hidden_ref.shape[1]

    barrier = pltpu.get_barrier_semaphore()
    for k in range(1, n_dp):
        pl.semaphore_signal(barrier, inc=1, device_id=(dp ^ k, fs), device_id_type=MESH)
    for k in range(1, n_fsdp):
        pl.semaphore_signal(barrier, inc=1, device_id=(dp, fs ^ k), device_id_type=MESH)
    pl.semaphore_wait(barrier, n_dp + n_fsdp - 2)

    def remote(out, into, send, recv, k, dst):
        return pltpu.make_async_remote_copy(
            src_ref=out,
            dst_ref=into.at[k],
            send_sem=send.at[k],
            recv_sem=recv.at[k],
            device_id=dst,
            device_id_type=MESH,
        )

    def x_copy(k):
        return remote(x_out.at[k], x_in, xs, xr, k, (dp ^ 1, fs))

    def z_copy(k):
        return remote(z_out.at[k], z_in, zs, zr, k, (dp ^ (4 * k), fs))

    def n_copy(k):
        return remote(n_out.at[k], n_in, ns, nr, k, (dp ^ 2, fs))

    def c_copy(j):
        return remote(c_out.at[j], c_in, cs, cr, j, (dp, fs ^ 1))

    def y_copy(j):
        return remote(y_out.at[j], y_in, ys, yr, j, (dp, (y ^ j) * 2 + c))

    def d_copy(j):
        return remote(d_out, d_in, ds_, dr, j, (dp, fs ^ j))

    def g_copy(k):
        return remote(g_out, g_in, gs, gr, k, (dp ^ k, fs))

    def dw(block):
        if feats % 128 == 0:
            left = normed_ref[:, pl.ds(pl.multiple_of(block * feats, 128), feats)]
        else:
            left = normed_ref[block]
        return lax.dot_general(
            left, dlogits_ref[...], (((0,), (0,)), ((), ())), preferred_element_type=jnp.float32
        )

    def dn(block):
        right = head_ref[:, pl.ds(pl.multiple_of(block * cols, 128), cols)]
        return jnp.dot(dlogits_ref[...], right, preferred_element_type=jnp.float32)

    @pl.loop(0, outer_dp)
    def _(i):
        k = outer_dp - 1 - i
        x_out[k] = dw((z ^ k) * 2 + (1 - x)).astype(jnp.bfloat16)
        x_copy(k).start()

    @pl.loop(0, outer_fs)
    def _(i):
        j = outer_fs - 1 - i
        c_out[j] = dn((y ^ j) * 2 + (1 - c)).astype(jnp.bfloat16)
        c_copy(j).start()

    @pl.loop(0, outer_fs - 1)
    def _(i):
        j = outer_fs - 1 - i
        mine = dn((y ^ j) * 2 + c)
        c_copy(j).wait_recv()
        y_out[j] = (mine + c_in[j].astype(jnp.float32)).astype(jnp.bfloat16)
        y_copy(j).start()

    acc[...] = dn(fs)
    c_copy(0).wait_recv()
    acc[...] += c_in[0].astype(jnp.float32)

    def pair_sum(k):
        mine = dw((z ^ k) * 2 + x)
        x_copy(k).wait_recv()
        return mine + x_in[k].astype(jnp.float32)

    def to_near(q):
        n_out[q] = pair_sum(2 * q + 1).astype(jnp.bfloat16)
        n_copy(q).start()

    @pl.loop(0, quads - 1)
    def _(i):
        q = quads - 1 - i
        to_near(q)
        mine = pair_sum(2 * q)
        n_copy(q).wait_recv()
        z_out[q] = (mine + n_in[q].astype(jnp.float32)).astype(jnp.bfloat16)
        z_copy(q).start()

    to_near(0)

    @pl.loop(1, outer_fs)
    def _(j):
        y_copy(j).wait_recv()
        acc[...] += y_in[j].astype(jnp.float32)

    h = hidden_ref[...].astype(jnp.float32)
    inv = inv_ref[...]
    g_out[:, :cols] = jnp.broadcast_to(
        jnp.sum(acc[...] * h * inv, axis=0, keepdims=True), (8, cols)
    )
    g_out[:, cols:] = loss_ref[...]

    @pl.loop(1, n_dp)
    def _(k):
        g_copy(k).start()

    dy = acc[...] * gain_ref[...]
    part = jnp.sum(h * dy, axis=1, keepdims=True)
    rows = part.shape[0]
    d_out[...] = jnp.transpose(jnp.broadcast_to(part, (rows, 128)))[:8]
    for j in range(1, n_fsdp):
        d_copy(j).start()
    dots = d_out[...]
    for j in range(1, n_fsdp):
        d_copy(j).wait_recv()
        dots += d_in[j]
    column = jnp.transpose(jnp.broadcast_to(dots[:1], (128, rows)))[:, :1]
    scale = inv * inv * inv * column / (cols * n_fsdp)
    gh_ref[...] = (
        inv * (acc[...] * gain_ref[...]) - hidden_ref[...].astype(jnp.float32) * scale
    ).astype(jnp.bfloat16)

    gg_ref[...] = g_out[...]

    @pl.loop(1, n_dp)
    def _(k):
        g_copy(k).wait_recv()
        gg_ref[...] += g_in[k]

    gw_ref[...] = pair_sum(0)
    n_copy(0).wait_recv()
    gw_ref[...] += n_in[0].astype(jnp.float32)

    @pl.loop(1, quads)
    def _(k):
        z_copy(k).wait_recv()
        gw_ref[...] += z_in[k].astype(jnp.float32)

    @pl.loop(0, outer_dp)
    def _(k):
        x_copy(k).wait_send()

    @pl.loop(0, quads)
    def _(k):
        n_copy(k).wait_send()

    @pl.loop(1, quads)
    def _(k):
        z_copy(k).wait_send()

    @pl.loop(0, outer_fs)
    def _(j):
        c_copy(j).wait_send()

    @pl.loop(1, outer_fs)
    def _(j):
        y_copy(j).wait_send()

    for j in range(1, n_fsdp):
        d_copy(j).wait_send()

    @pl.loop(1, n_dp)
    def _(k):
        g_copy(k).wait_send()


def tail(normed, dlogits, head, hidden, gain_row, inv, loss_tile):
    n_dp, n_fsdp = lax.axis_size("dp"), lax.axis_size("fsdp")
    rows, width = normed.shape
    vocab_here = head.shape[0]
    cols = hidden.shape[1]
    feats = width // n_dp
    zd, qd, yd = n_dp // 2, n_dp // 4, n_fsdp // 2
    if feats % 128:
        normed = normed.reshape(rows, n_dp, feats).transpose(1, 0, 2)
    wide = cols + 128
    bf, f32 = jnp.bfloat16, jnp.float32
    vm = pl.BlockSpec(memory_space=pltpu.VMEM)
    dma = pltpu.SemaphoreType.DMA
    return pl.pallas_call(
        functools.partial(tail_kernel, n_dp, n_fsdp, feats),
        out_shape=(
            jax.ShapeDtypeStruct((rows, cols), bf),
            jax.ShapeDtypeStruct((feats, vocab_here), f32),
            jax.ShapeDtypeStruct((8, wide), f32),
        ),
        in_specs=[vm] * 7,
        out_specs=(vm, vm, vm),
        scratch_shapes=[
            pltpu.VMEM((zd, feats, vocab_here), bf),
            pltpu.VMEM((zd, feats, vocab_here), bf),
            pltpu.VMEM((qd, feats, vocab_here), bf),
            pltpu.VMEM((qd, feats, vocab_here), bf),
            pltpu.VMEM((qd, feats, vocab_here), bf),
            pltpu.VMEM((qd, feats, vocab_here), bf),
            pltpu.VMEM((yd, rows, cols), bf),
            pltpu.VMEM((yd, rows, cols), bf),
            pltpu.VMEM((yd, rows, cols), bf),
            pltpu.VMEM((yd, rows, cols), bf),
            pltpu.VMEM((rows, cols), f32),
            pltpu.VMEM((8, rows), f32),
            pltpu.VMEM((n_fsdp, 8, rows), f32),
            pltpu.VMEM((8, wide), f32),
            pltpu.VMEM((n_dp, 8, wide), f32),
        ]
        + [dma((n,)) for n in (zd, zd, qd, qd, qd, qd, yd, yd, yd, yd, n_fsdp, n_fsdp, n_dp, n_dp)],
        compiler_params=pltpu.CompilerParams(
            collective_id=0, has_side_effects=True, vmem_limit_bytes=60 * 1024 * 1024
        ),
    )(normed, dlogits, head, hidden, gain_row, inv, loss_tile)


def body(hidden, gain, head, targets, lengths, old_logp, rewards, group_slot):
    resp_here, length_max, shard_cols = hidden.shape
    rows = resp_here * length_max
    whole, gain_full = (
        lax.all_gather(hidden, "fsdp", axis=2, tiled=True),
        lax.all_gather(gain, "fsdp", axis=0, tiled=True),
    )
    width = whole.shape[2]
    whole = whole.reshape(rows, width)
    vocab_here = head.shape[0]
    vocab_start = lax.axis_index("fsdp") * vocab_here
    groups_all = resp_here * lax.axis_size("dp") // GROUP
    group = group_slot // GROUP
    member = (group[:, None] == jnp.arange(groups_all, dtype=jnp.int32)[None, :]).astype(
        jnp.float32
    )
    local_sums = jnp.sum(member * rewards[:, None], axis=0)
    local_count = jnp.sum(lengths).astype(jnp.float32)
    group_sums, count = lax.psum((local_sums, local_count), "dp")
    adv_resp = rewards - jnp.sum(member * group_sums[None, :], axis=1) / GROUP
    adv = jnp.repeat(adv_resp, length_max)
    mask = (
        (jnp.arange(length_max, dtype=jnp.int32)[None, :] < lengths[:, None])
        .astype(jnp.float32)
        .reshape(rows)
    )
    gain_f = gain_full.astype(jnp.float32)
    inv = lax.rsqrt(
        jnp.mean(jnp.square(whole.astype(jnp.float32)), axis=1, keepdims=True) + eps_norm
    )
    normed = (whole.astype(jnp.float32) * inv * gain_f).astype(jnp.bfloat16)
    logits = lax.dot_general(
        normed, head, (((1,), (1,)), ((), ())), preferred_element_type=jnp.float32
    )
    top_local = jnp.max(logits, axis=1)
    sum_local = jnp.sum(jnp.exp(logits - top_local[:, None]), axis=1)
    local_targets = targets.reshape(rows) - vocab_start
    hits = jnp.arange(vocab_here, dtype=jnp.int32)[None, :] == local_targets[:, None]
    chosen_local = jnp.sum(jnp.where(hits, logits, 0.0), axis=1)
    stats = lax.all_gather(jnp.stack([top_local, sum_local, chosen_local]), "fsdp", axis=0)
    top = jnp.max(stats[:, 0], axis=0)
    total = jnp.sum(stats[:, 1] * jnp.exp(stats[:, 0] - top[None, :]), axis=0)
    chosen = jnp.sum(stats[:, 2], axis=0)
    lse = top + jnp.log(total)
    logp = chosen - lse
    ratio = jnp.exp(logp - old_logp.reshape(rows))
    first = ratio * adv
    second = jnp.clip(ratio, clip_low, clip_high) * adv
    policy = -jnp.minimum(first, second)
    policy = jnp.where(adv < 0, jnp.minimum(policy, -dual_bound * adv), policy)
    loss_local = jnp.sum(mask * policy)
    active = (first <= second) & jnp.logical_not((adv < 0) & (first < dual_bound * adv))
    slots_all = rows * lax.axis_size("dp")
    grad_logp = slots_all / count * mask * jnp.where(active, -ratio * adv, 0.0)
    probs = jnp.exp(logits - lse[:, None])
    dlogits = (grad_logp[:, None] * (hits.astype(jnp.float32) - probs)).astype(jnp.bfloat16)
    grad_h, grad_head_t, sums = tail(
        normed,
        dlogits,
        head,
        hidden.reshape(rows, shard_cols),
        gain.astype(jnp.float32)[None, :],
        inv,
        jnp.broadcast_to(loss_local, (8, 128)),
    )
    loss = sums[0, shard_cols] / count
    grad_gain = sums[0, :shard_cols]
    grad_hidden = grad_h.reshape(resp_here, length_max, shard_cols)
    return (loss, grad_hidden, grad_gain, grad_head_t)


def solution(mesh):
    in_specs = (
        P("dp", None, "fsdp"),
        P("fsdp"),
        P("fsdp", None),
        P("dp", None),
        P("dp"),
        P("dp", None),
        P("dp"),
        P("dp"),
    )
    out_specs = (P(), P("dp", None, "fsdp"), P("fsdp"), P("dp", "fsdp"))
    return jax.shard_map(body, mesh=mesh, in_specs=in_specs, out_specs=out_specs, check_vma=False)
```

profile of v0, /device:TPU:0, one launch (start us, length us, event | category | flops | bytes accessed | tf_op | source)
XLA Modules:
  0.0 180.4 jit_solution(10985499645446271927)
XLA Ops:
  7.2 0.0 all-gather.5.cloned.1.call-start
  7.2 0.7 all-gather.5.cloned.1.call-update
  7.9 1.3 reduce_sum.82
  9.2 0.7 and_select_fusion
  9.9 0.7 select_reduce_fusion.2
  11.2 23.6 %all-reduce = (f32[]{:T(128)}, f32[2]{0:T(128)S(1)}) all-reduce(f32[]{:T(128)S(6)} %convert_element_type.36, f32[2]{0:T(128)S(1)} %select_reduce_fusion.2), channel_id=1, replica_groups=mesh['dp'=8,'fsdp'=4] {'dp'}, use_global_device_ids=true, to_apply=%region_2.3 | all-reduce | flops 3 | bytes 24 | tf_op jit(solution)/shard_map/psum | solution.py:307
  34.9 0.7 reshape.149
  35.6 1.3 reshape.147.gain_ref
  36.9 5.4 %all-gather.1 = bf16[4,1,1280]{2,1,0:T(2,128)(2,1)S(1)} all-gather(bf16[1,1,1280]{2,1,0:T(2,128)(2,1)S(1)} %reshape.149), channel_id=1, replica_groups=mesh['dp'=8,'fsdp'=4] {'fsdp'}, dimensions={0}, use_global_device_ids=true | all-gather | bytes 12800 | tf_op jit(solution)/shard_map/all_gather | solution.py:294
  42.3 0.7 subtract_bitcast_fusion
  43.0 0.2 select_reduce_fusion.1
  43.2 0.7 broadcast_multiply_fusion
  43.8 0.1 broadcast_bitcast_fusion
  44.6 0.7 select_bitcast_fusion
  45.3 0.7 copy.32
  46.0 6.8 %all-gather.5.cloned.1.call-done = bf16[2,256,5120]{2,1,0:T(8,128)(2,1)} async-done(((bf16[2,256,1280]{2,1,0:T(8,128)(2,1)}), bf16[2,256,5120]{2,1,0:T(8,128)(2,1)}) %all-gather.5.cloned.1.call-update) | async-done | bytes 5242896 | tf_op jit(solution)/shard_map/all_gather | solution.py:293
  52.8 0.0 copy-start
  52.8 0.0 slice-start
  52.8 3.7 %multiply_reduce_fusion = f32[2,256]{1,0:T(2,128)S(1)} fusion(bf16[2,256,5120]{2,1,0:T(8,128)(2,1)} %all-gather.5.cloned.1.call-done), kind=kLoop, calls=%fused_computation.3 | loop fusion | flops 7863808 | bytes 5244928 | tf_op jit(solution)/shard_map/reduce_sum | solution.py:317
  56.6 0.3 copy-done
  56.9 0.0 slice-start.1
  56.9 2.0 %fusion.1.normed_ref = bf16[512,5120]{1,0:T(8,128)(2,1)S(1)} fusion(f32[5120]{0:T(1024)S(1)} %bitcast.53, f32[512]{0:T(512)S(1)} %bitcast.64, bf16[2,256,5120]{2,1,0:T(8,128)(2,1)S(1)} %copy-done), kind=kLoop, calls=%fused_computation.2 | loop fusion | flops 10485760 | bytes 10508288 | tf_op jit(solution)/shard_map/convert_element_type | solution.py:319
  58.9 0.0 slice-done
  58.9 0.0 slice-done.1
  58.9 0.0 copy-start.1
  58.9 2.9 %fusion.11 = (f32[512]{0:T(512)S(1)}, f32[512,512]{0,1:T(8,128)S(1)}) fusion(bf16[512,5120]{1,0:T(8,128)(2,1)S(1)} %fusion.1.normed_ref, bf16[512,5120]{1,0:T(8,128)(2,1)S(1)} %bitcast.49), kind=kOutput, calls=%fused_computation.44 | convolution fusion | flops 2684616192 | bytes 11536384 | tf_op jit(solution)/shard_map/dot_general | solution.py:320
  61.8 0.0 copy-done.1
  61.8 0.0 copy-start.2
  61.9 0.0 copy-start.3
  61.9 0.3 copy.23
  62.2 0.2 exponential_reduce_fusion
  62.4 0.3 select_reduce_fusion
  62.7 5.4 %all-gather.2 = f32[4,3,512]{2,1,0:T(4,128)S(1)} all-gather(f32[1,3,512]{2,1,0:T(4,128)S(1)} %maximum_bitcast_fusion), channel_id=2, replica_groups=mesh['dp'=8,'fsdp'=4] {'fsdp'}, dimensions={0}, use_global_device_ids=true | all-gather | bytes 30720 | tf_op jit(solution)/shard_map/all_gather | solution.py:328
  68.2 0.9 copy.35
  69.0 1.1 multiply_convert_fusion.dlogits_ref
  70.2 0.0 copy-done.2
  70.2 0.0 copy-done.3
  70.2 0.7 fusion.8
  70.9 1.2 broadcast_in_dim.41.loss_ref
  72.1 91.5 %shard_map.111 = (bf16[512,1280]{1,0:T(8,128)(2,1)}, f32[640,512]{1,0:T(8,128)}, f32[8,1408]{1,0:T(8,128)}) custom-call(bf16[512,5120]{1,0:T(8,128)(2,1)} %copy-done.1, bf16[512,512]{1,0:T(8,128)(2,1)} %multiply_convert_fusion.dlogits_ref, bf16[512,5120]{1,0:T(8,128)(2,1)} %head_ref.1, bf16[512,1280]{1,0:T(8,128)(2,1)} %bitcast.50, ...), custom_call_target="tpu_custom_call" | custom-call | tf_op jit(solution)/shard_map/pallas_call | solution.py:256
  163.6 1.4 slice_reduce_fusion.1
  165.0 1.2 slice.19
  167.5 2.5 %copy.44 = bf16[2,256,1280]{2,1,0:T(8,128)(2,1)} copy(bf16[2,256,1280]{2,1,0:T(8,128)(2,1)} %bitcast.51) | data formatting | bytes 2621440
  170.0 2.5 %copy.45 = f32[640,512]{1,0:T(8,128)} copy(f32[640,512]{1,0:T(8,128)} %get-tuple-element.32) | data formatting | bytes 2621440
  (14 shorter events, 0.2 us)
Async XLA Ops:
  7.2 45.6 %all-gather.5.cloned.1.call-start = ((), (), s32[]{:S(2)}) async-start(), calls=%async_computation | async-start | bytes 6553600 | tf_op jit(solution)/shard_map/all_gather | solution.py:293
  52.8 4.0 %copy-start = (bf16[2,256,5120]{2,1,0:T(8,128)(2,1)S(1)}, bf16[2,256,5120]{2,1,0:T(8,128)(2,1)}, u32[]{:S(2)}) copy-start(bf16[2,256,5120]{2,1,0:T(8,128)(2,1)} %all-gather.5.cloned.1.call-done) | copy-start | bytes 15728644
  52.8 6.1 %slice-start = ((s8[5242880]{0:T(1024)(128)(4,1)}), s8[4194304]{0:T(1024)(128)(4,1)S(1)}, s32[]{:S(2)}) async-start(s8[5242880]{0:T(1024)(128)(4,1)} %bitcast.48), calls=%async_computation.1 | async-start | bytes 8388608
  56.9 2.0 %slice-start.1 = ((s8[5242880]{0:T(1024)(128)(4,1)}), s8[1048576]{0:T(1024)(128)(4,1)S(1)}, s32[]{:S(2)}) async-start(s8[5242880]{0:T(1024)(128)(4,1)} %bitcast.48), calls=%async_computation.2 | async-start | bytes 2097152
  58.9 2.9 %copy-start.1 = (bf16[512,5120]{1,0:T(8,128)(2,1)}, bf16[512,5120]{1,0:T(8,128)(2,1)S(1)}, u32[]{:S(2)}) copy-start(bf16[512,5120]{1,0:T(8,128)(2,1)S(1)} %fusion.1.normed_ref) | copy-start | bytes 15728644
  61.8 8.3 %copy-start.2 = (f32[2,256]{1,0:T(2,128)S(1)}, f32[2,256]{1,0:T(2,128)}, u32[]{:S(2)}) copy-start(f32[2,256]{1,0:T(2,128)} %param.13) | copy-start | bytes 6148
  61.9 8.3 %copy-start.3 = (s32[2]{0:T(128)S(1)}, s32[2]{0:T(128)}, u32[]{:S(2)}) copy-start(s32[2]{0:T(128)} %param.12) | copy-start | bytes 28
Sparse Core Ops, SparseCore 0:
  9.5 43.2 all-gather.4
where the time goes:
time: 181 us; the launch traced here: 180 us
  Pallas kernels  91.5 us (51%)
  blocking collectives  34.4 us (19%)
  between operations  18 us (10%)
  other arithmetic  13.1 us (7%)
  local copies, waits for them, and re-layouts  13 us (7%)
  waiting for transfers between devices  7.47 us (4%)
  matrix products  2.91 us (2%)
    pallas_call x1, Pallas kernels, tail(): pl.pallas_call(functools.partial(tail_kernel, n_dp, n_fsdp, feats), out_s...  91.5 us
    psum x1, blocking collectives, body(): group_sums, count = lax.psum((local_sums, local_count), 'dp')  23.6 us
    unnamed x23, local copies, waits for them, and re-layouts  7.56 us
    all_gather x1, waiting for transfers between devices, body(): lax.all_gather(hidden, 'fsdp', axis=2, tiled=True)  6.79 us
    all_gather x1, blocking collectives, body(): lax.all_gather(gain, 'fsdp', axis=0, tiled=True)  5.42 us
    all_gather x1, blocking collectives, body(): lax.all_gather(jnp.stack([top_local, sum_local, chosen_local]), 'fsdp', a...  5.37 us
    reduce_sum x1, other arithmetic, body(): jnp.mean(jnp.square(whole.astype(jnp.float32)), axis=1, keepdims=True)  3.74 us
  transfers between devices with their start and end apart: 1, of which 1 were waited for; matrix products, arithmetic and copies ran while one was open for 4% of the time, Pallas kernels for 0%

commit v1 on v0

--- a/solution.py
+++ b/solution.py
@@ -7,6 +7,7 @@
 from jax.sharding import PartitionSpec as P
 
 GROUP = 8
+LANES = 128
 
 
 eps_norm = 1e-06
@@ -16,6 +17,535 @@
 
 
 MESH = pl.DeviceIdType.MESH
+
+
+def whole_kernel(
+    n_dp,
+    n_fsdp,
+    length_max,
+    small_ref,
+    hidden_ref,
+    head_hbm,
+    gh_ref,
+    gw_ref,
+    gg_ref,
+    head,
+    hs,
+    hz,
+    nm,
+    lg,
+    inv_s,
+    rowv,
+    cnt,
+    loss_s,
+    gain_in,
+    meta_out,
+    meta_in,
+    st_out,
+    st_in,
+    dls,
+    dlz,
+    c_out,
+    c_in,
+    y_out,
+    y_in,
+    acc,
+    d_out,
+    d_in,
+    x_out,
+    x_in,
+    z_out,
+    z_in,
+    fin,
+    g_out,
+    g_in,
+    own_sem,
+    head_sem,
+    ysem,
+    nsem,
+    fsem,
+    zsem,
+    wsem,
+    ssem,
+    msem,
+    tsem,
+    lsem,
+    csem,
+    rsem,
+    dsem,
+    xsem,
+    hsem,
+    gsem,
+):
+    dp = lax.axis_index("dp")
+    fs = lax.axis_index("fsdp")
+    zh, zl, x = dp // 4, (dp // 2) % 2, dp % 2
+    y, c = fs // 2, fs % 2
+    rows, cols = hidden_ref.shape
+    voc = head_hbm.shape[0]
+    nch = rows // LANES
+    half = LANES // 2
+    feats = gw_ref.shape[0]
+    groups_all = rows // length_max * n_dp // GROUP
+    f32, bf = jnp.float32, jnp.bfloat16
+    pick = (c + 1 - zl) % 2
+
+    def span(i):
+        return pl.ds(pl.multiple_of(i * LANES, LANES), LANES)
+
+    def shard(j):
+        return pl.ds(pl.multiple_of((fs ^ j) * cols, LANES), cols)
+
+    def remote(src, dst, sems, at, to):
+        return pltpu.make_async_remote_copy(
+            src_ref=src,
+            dst_ref=dst,
+            send_sem=sems.at[(0, *at)],
+            recv_sem=sems.at[(1, *at)],
+            device_id=to,
+            device_id_type=MESH,
+        )
+
+    core, across = (dp, fs ^ 1), (dp, fs ^ 2)
+    near, side, far = (dp ^ 2, fs), (dp ^ 1, fs), (dp ^ 4, fs)
+
+    def own_copy(i):
+        return pltpu.make_async_copy(hidden_ref.at[span(i)], hs.at[0, span(i)], own_sem.at[i])
+
+    head_copy = pltpu.make_async_copy(head_hbm, head, head_sem.at[0])
+
+    def y_copy(i):
+        return remote(hs.at[0, span(i)], hs.at[2, span(i)], ysem, (i,), across)
+
+    def n_copy(i):
+        return remote(hs.at[0, span(i)], hs.at[1, span(i)], nsem, (i,), core)
+
+    def f_copy(i):
+        return remote(hs.at[2, span(i)], hs.at[3, span(i)], fsem, (i,), core)
+
+    def z_copy(k, i):
+        part = pl.ds(pl.multiple_of(i * LANES + c * half, half), half)
+        return remote(hs.at[2 * k + pick, part], hz.at[k, part], zsem, (k, i), near)
+
+    def w_copy(k, i):
+        part = pl.ds(pl.multiple_of(i * LANES + c * half, half), half)
+        return remote(hz.at[k, part], hz.at[k, part], wsem, (k, i), core)
+
+    def s_copy(j):
+        return remote(small_ref, gain_in.at[j], ssem, (j,), (dp, fs ^ j))
+
+    def m_copy(k):
+        return remote(meta_out, meta_in.at[k], msem, (k,), (dp ^ k, fs))
+
+    def t_copy(j, i):
+        return remote(st_out.at[i], st_in.at[j, i], tsem, (j, i), (dp, fs ^ j))
+
+    def l_copy(i):
+        return remote(dls.at[i], dlz.at[i], lsem, (i,), near)
+
+    def c_copy(k, i):
+        return remote(c_out.at[k, span(i)], c_in.at[k, span(i)], csem, (k, i), core)
+
+    def r_copy(i):
+        return remote(y_out.at[span(i)], y_in.at[span(i)], rsem, (i,), across)
+
+    def d_copy(j, i):
+        return remote(d_out.at[i], d_in.at[j, i], dsem, (j, i), (dp, fs ^ j))
+
+    def x_copy(k, p):
+        return remote(x_out.at[k, span(p)], x_in.at[k, span(p)], xsem, (k, p), side)
+
+    def h_copy(p):
+        return remote(z_out.at[span(p)], z_in.at[span(p)], hsem, (p,), far)
+
+    def g_copy(k):
+        return remote(g_out, g_in.at[k], gsem, (k,), (dp ^ k, fs))
+
+    for i in range(nch):
+        own_copy(i).start()
+    head_copy.start()
+
+    barrier = pltpu.get_barrier_semaphore()
+    for k in range(1, n_dp):
+        pl.semaphore_signal(barrier, inc=1, device_id=(dp ^ k, fs), device_id_type=MESH)
+    for k in range(1, n_fsdp):
+        pl.semaphore_signal(barrier, inc=1, device_id=(dp, fs ^ k), device_id_type=MESH)
+    pl.semaphore_wait(barrier, n_dp + n_fsdp - 2)
+
+    @pl.loop(0, nch)
+    def _(i):
+        own_copy(i).wait()
+        y_copy(i).start()
+        n_copy(i).start()
+
+    for j in range(1, n_fsdp):
+        s_copy(j).start()
+
+    reward = small_ref[4:5, :rows]
+    group = small_ref[5:6, :rows]
+    lens = small_ref[3:4, :rows]
+    place = lax.broadcasted_iota(jnp.int32, (1, rows), 1) % length_max
+    first_here = place == 0
+    lane = lax.broadcasted_iota(jnp.int32, (8, LANES), 1)
+    tile = jnp.where(
+        lane == groups_all, jnp.sum(jnp.where(first_here, lens, 0.0), axis=1, keepdims=True), 0.0
+    )
+    for g in range(groups_all):
+        mine = jnp.where(first_here & (group == float(g)), reward, 0.0)
+        tile = jnp.where(lane == g, jnp.sum(mine, axis=1, keepdims=True), tile)
+    meta_out[...] = tile
+    for k in range(1, n_dp):
+        m_copy(k).start()
+
+    loss_s[...] = jnp.zeros_like(loss_s)
+    g_out[...] = jnp.zeros_like(g_out)
+    head_copy.wait()
+
+    @pl.loop(0, nch)
+    def _(i):
+        n_copy(i).wait_recv()
+        z_copy(0, i).start()
+
+    gain_in[0] = small_ref[...]
+    for j in range(1, n_fsdp):
+        s_copy(j).wait_recv()
+    total = meta_out[...]
+    for k in range(1, n_dp):
+        m_copy(k).wait_recv()
+        total += meta_in[k]
+
+    def entry(g):
+        return jnp.sum(jnp.where(lane == g, total, 0.0), axis=1, keepdims=True)[:1]
+
+    mean = jnp.zeros((1, rows), f32)
+    for g in range(groups_all):
+        mean = jnp.where(group == float(g), entry(g) / GROUP, mean)
+    rowv[0:1] = reward - mean
+    rowv[1:2] = jnp.where(place.astype(f32) < lens, 1.0, 0.0)
+    cnt[...] = jnp.broadcast_to(entry(groups_all), cnt.shape)
+    slots_all = rows * n_dp
+
+    def hits_of(i):
+        at = lax.broadcasted_iota(jnp.int32, (voc, LANES), 0) + fs * voc
+        return at.astype(f32) == small_ref[1:2, span(i)]
+
+    def forward(i):
+        y_copy(i).wait_recv()
+        f_copy(i).start()
+        z_copy(0, i).wait_recv()
+        w_copy(0, i).start()
+        square = jnp.zeros((LANES, 1), f32)
+        for j in range(3):
+            h = hs[j, span(i)].astype(f32)
+            square += jnp.sum(h * h, axis=1, keepdims=True)
+        f_copy(i).wait_recv()
+        z_copy(1, i).start()
+        h = hs[3, span(i)].astype(f32)
+        square += jnp.sum(h * h, axis=1, keepdims=True)
+        inv = lax.rsqrt(square / (cols * n_fsdp) + eps_norm)
+        inv_s[span(i)] = inv
+        for j in range(n_fsdp):
+            nm[j] = (hs[j, span(i)].astype(f32) * inv * gain_in[j, 0:1, :cols]).astype(bf)
+        lg[i] = jnp.zeros((voc, LANES), f32)
+
+        @pl.loop(0, n_fsdp)
+        def _(j):
+            lg[i] += lax.dot_general(
+                head[:, shard(j)], nm[j], (((1,), (1,)), ((), ())), preferred_element_type=f32
+            )
+
+        logits = lg[i]
+        top = jnp.max(logits, axis=0, keepdims=True)
+        st_out[i, 0:1] = top
+        st_out[i, 1:2] = jnp.sum(jnp.exp(logits - top), axis=0, keepdims=True)
+        st_out[i, 2:3] = jnp.sum(jnp.where(hits_of(i), logits, 0.0), axis=0, keepdims=True)
+        st_out[i, 3:8] = jnp.zeros((5, LANES), f32)
+        for j in range(1, n_fsdp):
+            t_copy(j, i).start()
+
+    def backward(i):
+        for j in range(1, n_fsdp):
+            t_copy(j, i).wait_recv()
+        stats = [st_out[i]] + [st_in[j, i] for j in range(1, n_fsdp)]
+        top = stats[0][0:1]
+        for s in stats[1:]:
+            top = jnp.maximum(top, s[0:1])
+        total = jnp.zeros_like(top)
+        chosen = jnp.zeros_like(top)
+        for s in stats:
+            total += s[1:2] * jnp.exp(s[0:1] - top)
+            chosen += s[2:3]
+        lse = top + jnp.log(total)
+        adv, mask = rowv[0:1, span(i)], rowv[1:2, span(i)]
+        ratio = jnp.exp(chosen - lse - small_ref[2:3, span(i)])
+        first = ratio * adv
+        second = jnp.clip(ratio, clip_low, clip_high) * adv
+        policy = -jnp.minimum(first, second)
+        policy = jnp.where(adv < 0, jnp.minimum(policy, -dual_bound * adv), policy)
+        loss_s[0:1] += mask * policy
+        active = (first <= second) & jnp.logical_not((adv < 0) & (first < dual_bound * adv))
+        slope = slots_all / cnt[0:1] * mask * jnp.where(active, -ratio * adv, 0.0)
+        grad = slope * (hits_of(i).astype(f32) - jnp.exp(lg[i] - lse))
+        inv_row = jnp.transpose(jnp.broadcast_to(inv_s[span(i)], (LANES, LANES)))[:1]
+        dls[i] = (grad * inv_row).astype(bf)
+        l_copy(i).start()
+        left = jnp.transpose(grad).astype(bf)
+
+        def dn(j):
+            return jnp.dot(left, head[:, shard(j)], preferred_element_type=f32)
+
+        c_out[1, span(i)] = dn(3).astype(bf)
+        c_copy(1, i).start()
+        c_out[0, span(i)] = dn(1).astype(bf)
+        c_copy(0, i).start()
+        z_copy(1, i).wait_recv()
+        w_copy(1, i).start()
+        acc[span(i)] = dn(2)
+        c_copy(1, i).wait_recv()
+        y_out[span(i)] = (acc[span(i)] + c_in[1, span(i)].astype(f32)).astype(bf)
+        r_copy(i).start()
+        acc[span(i)] = dn(0)
+        c_copy(0, i).wait_recv()
+        acc[span(i)] += c_in[0, span(i)].astype(f32)
+
+    @pl.loop(0, nch + 1)
+    def _(i):
+        @pl.when(i < nch)
+        def _():
+            forward(i)
+
+        @pl.when(i > 0)
+        def _():
+            backward(i - 1)
+
+    def dots(i):
+        r_copy(i).wait_recv()
+        grad = acc[span(i)] + y_in[span(i)].astype(f32)
+        acc[span(i)] = grad
+        h = hs[0, span(i)].astype(f32)
+        prod = grad * h
+        g_out[:, :cols] += jnp.sum((prod * inv_s[span(i)]).reshape(LANES // 8, 8, cols), axis=0)
+        part = jnp.sum(prod * gain_in[0, 0:1, :cols], axis=1, keepdims=True)
+        d_out[i] = jnp.transpose(jnp.broadcast_to(part, (LANES, LANES)))[:8]
+        for j in range(1, n_fsdp):
+            d_copy(j, i).start()
+
+    def finish(i):
+        whole = d_out[i]
+        for j in range(1, n_fsdp):
+            d_copy(j, i).wait_recv()
+            whole += d_in[j, i]
+        column = jnp.transpose(jnp.broadcast_to(whole[:1], (LANES, LANES)))[:, :1]
+        inv = inv_s[span(i)]
+        scale = inv * inv * inv * column / (cols * n_fsdp)
+        gh_ref[span(i)] = (
+            inv * (acc[span(i)] * gain_in[0, 0:1, :cols])
+            - hs[0, span(i)].astype(f32) * scale
+        ).astype(bf)
+
+    def dw(p, zb, xb):
+        at = pl.ds(pl.multiple_of(xb * feats, LANES), feats)
+        left = jnp.concatenate([dls[i, span(p)] for i in range(nch)], axis=1)
+        other = jnp.concatenate([dlz[i, span(p)] for i in range(nch)], axis=1)
+        return jnp.dot(
+            left, hs[fs ^ (2 * zb + zl), :, at], preferred_element_type=f32
+        ) + jnp.dot(other, hz[y ^ zb, :, at], preferred_element_type=f32)
+
+    for i in range(nch):
+        l_copy(i).wait_recv()
+        w_copy(0, i).wait_recv()
+        w_copy(1, i).wait_recv()
+
+    @pl.loop(0, nch)
+    def _(p):
+        x_out[0, span(p)] = dw(p, 1 - zh, 1 - x).astype(bf)
+        x_copy(0, p).start()
+
+    @pl.loop(0, nch)
+    def _(p):
+        x_out[1, span(p)] = dw(p, zh, 1 - x).astype(bf)
+        x_copy(1, p).start()
+        dots(p)
+        fin[span(p)] = dw(p, 1 - zh, x)
+        x_copy(0, p).wait_recv()
+        z_out[span(p)] = (fin[span(p)] + x_in[0, span(p)].astype(f32)).astype(bf)
+        h_copy(p).start()
+        finish(p)
+
+    g_out[:, cols:] = loss_s[...]
+
+    @pl.loop(1, n_dp)
+    def _(k):
+        g_copy(k).start()
+
+    @pl.loop(0, nch)
+    def _(p):
+        fin[span(p)] = dw(p, zh, x)
+        x_copy(1, p).wait_recv()
+        fin[span(p)] += x_in[1, span(p)].astype(f32)
+
+    gg_ref[...] = g_out[...]
+
+    @pl.loop(1, n_dp)
+    def _(k):
+        g_copy(k).wait_recv()
+        gg_ref[...] += g_in[k]
+
+    gg_ref[:, cols:] = jnp.broadcast_to(
+        jnp.sum(gg_ref[0:1, cols:], axis=1, keepdims=True) / cnt[0:1], (8, LANES)
+    )
+    gg_ref[0:1, :cols] = jnp.sum(gg_ref[:, :cols], axis=0, keepdims=True)
+
+    mine = gain_in[fs ^ (2 * zh + zl), 0:1, pl.ds(pl.multiple_of(x * feats, LANES), feats)]
+    for p in range(nch):
+        h_copy(p).wait_recv()
+        piece = (fin[span(p)] + z_in[span(p)].astype(f32)) * mine
+        gw_ref[:, span(p)] = jnp.transpose(piece)
+
+    @pl.loop(0, nch)
+    def _(i):
+        y_copy(i).wait_send()
+        n_copy(i).wait_send()
+        f_copy(i).wait_send()
+        l_copy(i).wait_send()
+        r_copy(i).wait_send()
+        h_copy(i).wait_send()
+        for k in range(2):
+            z_copy(k, i).wait_send()
+            w_copy(k, i).wait_send()
+            c_copy(k, i).wait_send()
+            x_copy(k, i).wait_send()
+        for j in range(1, n_fsdp):
+            t_copy(j, i).wait_send()
+            d_copy(j, i).wait_send()
+
+    for j in range(1, n_fsdp):
+        s_copy(j).wait_send()
+
+    @pl.loop(1, n_dp)
+    def _(k):
+        m_copy(k).wait_send()
+        g_copy(k).wait_send()
+
+
+def whole(small, hidden, head, length_max):
+    n_dp, n_fsdp = lax.axis_size("dp"), lax.axis_size("fsdp")
+    rows, cols = hidden.shape
+    voc, width = head.shape
+    feats = width // n_dp
+    nch = rows // LANES
+    wide = cols + LANES
+    bf, f32 = jnp.bfloat16, jnp.float32
+    vm = pl.BlockSpec(memory_space=pltpu.VMEM)
+    anywhere = pl.BlockSpec(memory_space=pl.ANY)
+    dma = pltpu.SemaphoreType.DMA
+    return pl.pallas_call(
+        functools.partial(whole_kernel, n_dp, n_fsdp, length_max),
+        out_shape=(
+            jax.ShapeDtypeStruct((rows, cols), bf),
+            jax.ShapeDtypeStruct((feats, voc), f32),
+            jax.ShapeDtypeStruct((8, wide), f32),
+        ),
+        in_specs=[vm, anywhere, anywhere],
+        out_specs=(vm, vm, vm),
+        scratch_shapes=[
+            pltpu.VMEM((voc, width), bf),
+            pltpu.VMEM((n_fsdp, rows, cols), bf),
+            pltpu.VMEM((2, rows, cols), bf),
+            pltpu.VMEM((n_fsdp, LANES, cols), bf),
+            pltpu.VMEM((nch, voc, LANES), f32),
+            pltpu.VMEM((rows, 1), f32),
+            pltpu.VMEM((8, rows), f32),
+            pltpu.VMEM((8, LANES), f32),
+            pltpu.VMEM((8, LANES), f32),
+            pltpu.VMEM((n_fsdp, *small.shape), f32),
+            pltpu.VMEM((8, LANES), f32),
+            pltpu.VMEM((n_dp, 8, LANES), f32),
+            pltpu.VMEM((nch, 8, LANES), f32),
+            pltpu.VMEM((n_fsdp, nch, 8, LANES), f32),
+            pltpu.VMEM((nch, voc, LANES), bf),
+            pltpu.VMEM((nch, voc, LANES), bf),
+            pltpu.VMEM((2, rows, cols), bf),
+            pltpu.VMEM((2, rows, cols), bf),
+            pltpu.VMEM((rows, cols), bf),
+            pltpu.VMEM((rows, cols), bf),
+            pltpu.VMEM((rows, cols), f32),
+            pltpu.VMEM((nch, 8, LANES), f32),
+            pltpu.VMEM((n_fsdp, nch, 8, LANES), f32),
+            pltpu.VMEM((2, voc, feats), bf),
+            pltpu.VMEM((2, voc, feats), bf),
+            pltpu.VMEM((voc, feats), bf),
+            pltpu.VMEM((voc, feats), bf),
+            pltpu.VMEM((voc, feats), f32),
+            pltpu.VMEM((8, wide), f32),
+            pltpu.VMEM((n_dp, 8, wide), f32),
+            dma((nch,)),
+            dma((1,)),
+            dma((2, nch)),
+            dma((2, nch)),
+            dma((2, nch)),
+            dma((2, 2, nch)),
+            dma((2, 2, nch)),
+            dma((2, n_fsdp)),
+            dma((2, n_dp)),
+            dma((2, n_fsdp, nch)),
+            dma((2, nch)),
+            dma((2, 2, nch)),
+            dma((2, nch)),
+            dma((2, n_fsdp, nch)),
+            dma((2, 2, nch)),
+            dma((2, nch)),
+            dma((2, n_dp)),
+        ],
+        compiler_params=pltpu.CompilerParams(
+            collective_id=1, has_side_effects=True, vmem_limit_bytes=60 * 1024 * 1024
+        ),
+    )(small, hidden, head)
+
+
+def fits(hidden, head):
+    n_dp, n_fsdp = lax.axis_size("dp"), lax.axis_size("fsdp")
+    rows = hidden.shape[0] * hidden.shape[1]
+    voc, width = head.shape
+    return (
+        n_dp == 2 * n_fsdp
+        and n_fsdp == 2 * 2
+        and (width // n_dp) % LANES == 0
+        and rows % LANES == 0
+        and rows == voc
+        and rows <= hidden.shape[2]
+    )
+
+
+def body(hidden, gain, head, targets, lengths, old_logp, rewards, group_slot):
+    if not fits(hidden, head):
+        return general(hidden, gain, head, targets, lengths, old_logp, rewards, group_slot)
+    resp_here, length_max, cols = hidden.shape
+    rows = resp_here * length_max
+
+    def row(values):
+        flat = values.astype(jnp.float32).reshape(-1)
+        return jnp.pad(flat, (0, cols - flat.shape[0]))
+
+    def per_position(values):
+        return row(jnp.broadcast_to(values[:, None], (resp_here, length_max)))
+
+    small = jnp.stack(
+        [
+            row(gain),
+            row(targets),
+            row(old_logp),
+            per_position(lengths),
+            per_position(rewards),
+            per_position(group_slot // GROUP),
+            jnp.zeros((cols,), jnp.float32),
+            jnp.zeros((cols,), jnp.float32),
+        ]
+    )
+    grad_h, grad_head_t, sums = whole(small, hidden.reshape(rows, cols), head, length_max)
+    loss = sums[0, cols]
+    grad_gain = sums[0, :cols]
+    return (loss, grad_h.reshape(resp_here, length_max, cols), grad_gain, grad_head_t)
 
 
 def tail_kernel(
@@ -286,7 +816,7 @@
     )(normed, dlogits, head, hidden, gain_row, inv, loss_tile)
 
 
-def body(hidden, gain, head, targets, lengths, old_logp, rewards, group_slot):
+def general(hidden, gain, head, targets, lengths, old_logp, rewards, group_slot):
     resp_here, length_max, shard_cols = hidden.shape
     rows = resp_here * length_max
     whole, gain_full = (

time: 181 us -> 127 us (0.70)
  blocking collectives: 34.4 us -> 0 us
  Pallas kernels: 91.5 us -> 116 us
  between operations: 18 us -> 0.66 us
  other arithmetic: 13.1 us -> 2.01 us
  waiting for transfers between devices: 7.47 us -> 0 us
  local copies, waits for them, and re-layouts: 13 us -> 8.57 us
  matrix products: 2.91 us -> 0 us
    pallas_call x1, Pallas kernels: 91.5 us -> 116 us  [whole(): pl.pallas_call(functools.partial(whole_kernel, n_dp, n_fsdp, length_max),...]
    psum x1 -> x0, blocking collectives: 23.6 us -> none  [body(): group_sums, count = lax.psum((local_sums, local_count), 'dp')]
    all_gather x2 -> x0, blocking collectives: 10.8 us -> none  [the longest x1 5.42 us: body(): lax.all_gather(gain, 'fsdp', axis=0, tiled=True)]
    reduce_sum x9 -> x0, other arithmetic: 7.19 us -> none  [the longest x1 3.74 us: body(): jnp.mean(jnp.square(whole.astype(jnp.float32)), axis=1, keepdims=True)]
    all_gather x1 -> x0, waiting for transfers between devices: 6.79 us -> none  [body(): lax.all_gather(hidden, 'fsdp', axis=2, tiled=True)]
    unnamed x23 -> x14, local copies, waits for them, and re-layouts: 7.56 us -> 4.55 us
    dot_general x1 -> x0, matrix products: 2.91 us -> none  [body(): lax.dot_general(normed, head, (((1,), (1,)), ((), ())), preferred_element...]
    broadcast_in_dim x2 -> x0, local copies, waits for them, and re-layouts: 2.5 us -> none  [the longest x1 1.28 us: body(): gain.astype(jnp.float32)[None, :]]
  transfers between devices with their start and end apart: 1 -> 0, of which waited for: 1 -> 0; matrix products, arithmetic and copies ran while one was open for 4% -> 0% of each run, Pallas kernels for 0% -> 0%
where the time goes in v1:
time: 127 us
  Pallas kernels  116 us (91%)
  local copies, waits for them, and re-layouts  8.57 us (7%)
  other arithmetic  2.01 us (2%)
    pallas_call x1, Pallas kernels, whole(): pl.pallas_call(functools.partial(whole_kernel, n_dp, n_fsdp, length_max),...  116 us
    unnamed x14, local copies, waits for them, and re-layouts  4.55 us

profile of v1, /device:TPU:0, one launch (start us, length us, event | category | flops | bytes accessed | tf_op | source)
XLA Modules:
  0.0 127.0 jit_solution(9601577419119412344)
XLA Ops:
  0.6 0.0 copy-start
  0.6 0.7 convert_element_type.19
  1.3 0.1 broadcast_bitcast_fusion.2
  1.4 0.7 fusion
  2.1 0.1 broadcast_bitcast_fusion
  2.2 0.7 convert_bitcast_fusion
  2.9 0.0 copy-done
  2.9 0.1 broadcast_bitcast_fusion.1
  3.0 0.7 copy.13
  3.7 0.7 reshape.39
  4.4 0.7 stack.35.small_ref
  5.0 115.7 %shard_map.111 = (bf16[512,1280]{1,0:T(8,128)(2,1)}, f32[640,512]{1,0:T(8,128)}, f32[8,1408]{1,0:T(8,128)}) custom-call(f32[8,1280]{1,0:T(8,128)} %stack.35.small_ref, bf16[512,1280]{1,0:T(8,128)(2,1)} %bitcast.18, bf16[512,5120]{1,0:T(8,128)(2,1)} %head_hbm.1), custom_call_target="tpu_custom_call" | custom-call | tf_op jit(solution)/shard_map/pallas_call | solution.py:442
  120.8 1.4 %slice_reduce_fusion = f32[1280]{0:T(1024)} fusion(f32[8,1408]{1,0:T(8,128)} %get-tuple-element.7), kind=kLoop, calls=%fused_computation | loop fusion | bytes 10240 | tf_op jit(solution)/shard_map/slice | solution.py:547
  122.2 1.2 slice.6
  123.3 0.0 copy-start.1
  123.3 2.6 %copy.19 = bf16[2,256,1280]{2,1,0:T(8,128)(2,1)} copy(bf16[2,256,1280]{2,1,0:T(8,128)(2,1)} %bitcast.17) | data formatting | bytes 2621440
  125.9 0.0 copy-done.1
  125.9 1.1 copy.20
  (15 shorter events, 0.1 us)
Async XLA Ops:
  0.6 2.2 %copy-start = (f32[2]{0:T(128)S(1)}, f32[2]{0:T(128)}, u32[]{:S(2)}) copy-start(f32[2]{0:T(128)} %param.14) | copy-start | bytes 28
  123.3 2.6 %copy-start.1 = (f32[640,512]{1,0:T(8,128)S(1)}, f32[640,512]{1,0:T(8,128)}, u32[]{:S(2)}) copy-start(f32[640,512]{1,0:T(8,128)} %get-tuple-element.17) | copy-start | bytes 3932164

commit v2 on v1

--- a/solution.py
+++ b/solution.py
@@ -23,19 +23,32 @@
     n_dp,
     n_fsdp,
     length_max,
-    small_ref,
+    gain_ref,
+    targets_hbm,
+    old_hbm,
+    lengths_hbm,
+    rewards_hbm,
+    slots_hbm,
     hidden_ref,
     head_hbm,
     gh_ref,
     gw_ref,
     gg_ref,
+    targets,
+    old,
+    lengths,
+    rewards,
+    slots,
+    target_rows,
+    old_rows,
+    adv_rows,
+    mask_rows,
     head,
     hs,
     hz,
     nm,
     lg,
     inv_s,
-    rowv,
     cnt,
     loss_s,
     gain_in,
@@ -57,10 +70,12 @@
     z_out,
     z_in,
     fin,
+    gsum,
     g_out,
     g_in,
     own_sem,
     head_sem,
+    small_sem,
     ysem,
     nsem,
     fsem,
@@ -86,12 +101,16 @@
     nch = rows // LANES
     half = LANES // 2
     feats = gw_ref.shape[0]
-    groups_all = rows // length_max * n_dp // GROUP
+    resp_here = rows // length_max
+    groups_all = resp_here * n_dp // GROUP
     f32, bf = jnp.float32, jnp.bfloat16
     pick = (c + 1 - zl) % 2
 
     def span(i):
         return pl.ds(pl.multiple_of(i * LANES, LANES), LANES)
+
+    def piece(p):
+        return pl.ds(pl.multiple_of(p * half, half), half)
 
     def shard(j):
         return pl.ds(pl.multiple_of((fs ^ j) * cols, LANES), cols)
@@ -132,7 +151,7 @@
         return remote(hz.at[k, part], hz.at[k, part], wsem, (k, i), core)
 
     def s_copy(j):
-        return remote(small_ref, gain_in.at[j], ssem, (j,), (dp, fs ^ j))
+        return remote(gain_ref, gain_in.at[j], ssem, (j,), (dp, fs ^ j))
 
     def m_copy(k):
         return remote(meta_out, meta_in.at[k], msem, (k,), (dp ^ k, fs))
@@ -153,52 +172,64 @@
         return remote(d_out.at[i], d_in.at[j, i], dsem, (j, i), (dp, fs ^ j))
 
     def x_copy(k, p):
-        return remote(x_out.at[k, span(p)], x_in.at[k, span(p)], xsem, (k, p), side)
+        return remote(x_out.at[k, piece(p)], x_in.at[k, piece(p)], xsem, (k, p), side)
 
     def h_copy(p):
-        return remote(z_out.at[span(p)], z_in.at[span(p)], hsem, (p,), far)
+        return remote(z_out.at[piece(p)], z_in.at[piece(p)], hsem, (p,), far)
 
     def g_copy(k):
         return remote(g_out, g_in.at[k], gsem, (k,), (dp ^ k, fs))
-
-    for i in range(nch):
-        own_copy(i).start()
-    head_copy.start()
 
     barrier = pltpu.get_barrier_semaphore()
     for k in range(1, n_dp):
         pl.semaphore_signal(barrier, inc=1, device_id=(dp ^ k, fs), device_id_type=MESH)
     for k in range(1, n_fsdp):
         pl.semaphore_signal(barrier, inc=1, device_id=(dp, fs ^ k), device_id_type=MESH)
+    loads = [
+        pltpu.make_async_copy(src, dst, small_sem.at[n])
+        for n, (src, dst) in enumerate(
+            [
+                (slots_hbm, slots),
+                (rewards_hbm, rewards),
+                (lengths_hbm, lengths),
+                (targets_hbm, targets),
+                (old_hbm, old),
+            ]
+        )
+    ]
+    for load in loads:
+        load.start()
+    for i in range(nch):
+        own_copy(i).start()
+    head_copy.start()
+    for load in loads:
+        load.wait()
+
+    lane = lax.broadcasted_iota(jnp.int32, (8, LANES), 1)
+    tile = jnp.zeros((8, LANES), f32)
+    for r in range(resp_here):
+        tile += jnp.where(lane == slots[r] // GROUP, rewards[r], 0.0)
+        tile += jnp.where(lane == groups_all, lengths[r].astype(f32), 0.0)
+    meta_out[...] = tile
+
     pl.semaphore_wait(barrier, n_dp + n_fsdp - 2)
+
+    for j in range(1, n_fsdp):
+        s_copy(j).start()
+    for k in range(1, n_dp):
+        m_copy(k).start()
 
     @pl.loop(0, nch)
     def _(i):
         own_copy(i).wait()
-        y_copy(i).start()
         n_copy(i).start()
 
-    for j in range(1, n_fsdp):
-        s_copy(j).start()
-
-    reward = small_ref[4:5, :rows]
-    group = small_ref[5:6, :rows]
-    lens = small_ref[3:4, :rows]
-    place = lax.broadcasted_iota(jnp.int32, (1, rows), 1) % length_max
-    first_here = place == 0
-    lane = lax.broadcasted_iota(jnp.int32, (8, LANES), 1)
-    tile = jnp.where(
-        lane == groups_all, jnp.sum(jnp.where(first_here, lens, 0.0), axis=1, keepdims=True), 0.0
-    )
-    for g in range(groups_all):
-        mine = jnp.where(first_here & (group == float(g)), reward, 0.0)
-        tile = jnp.where(lane == g, jnp.sum(mine, axis=1, keepdims=True), tile)
-    meta_out[...] = tile
-    for k in range(1, n_dp):
-        m_copy(k).start()
+        @pl.when(i < 2)
+        def _():
+            y_copy(i).start()
 
     loss_s[...] = jnp.zeros_like(loss_s)
-    g_out[...] = jnp.zeros_like(g_out)
+    gsum[...] = jnp.zeros_like(gsum)
     head_copy.wait()
 
     @pl.loop(0, nch)
@@ -206,7 +237,7 @@
         n_copy(i).wait_recv()
         z_copy(0, i).start()
 
-    gain_in[0] = small_ref[...]
+    gain_in[0] = gain_ref[...]
     for j in range(1, n_fsdp):
         s_copy(j).wait_recv()
     total = meta_out[...]
@@ -217,17 +248,20 @@
     def entry(g):
         return jnp.sum(jnp.where(lane == g, total, 0.0), axis=1, keepdims=True)[:1]
 
-    mean = jnp.zeros((1, rows), f32)
-    for g in range(groups_all):
-        mean = jnp.where(group == float(g), entry(g) / GROUP, mean)
-    rowv[0:1] = reward - mean
-    rowv[1:2] = jnp.where(place.astype(f32) < lens, 1.0, 0.0)
+    for i in range(nch):
+        r, first = i * LANES // length_max, i * LANES % length_max
+        position = lax.broadcasted_iota(jnp.int32, (1, LANES), 1) + first
+        target_rows[i] = targets[r : r + 1, first : first + LANES]
+        old_rows[i] = old[r : r + 1, first : first + LANES]
+        mask_rows[i] = jnp.where(position < lengths[r], 1.0, 0.0)
+        adv = rewards[r] - entry(slots[r] // GROUP) / GROUP
+        adv_rows[i] = jnp.broadcast_to(adv, (1, LANES))
     cnt[...] = jnp.broadcast_to(entry(groups_all), cnt.shape)
     slots_all = rows * n_dp
 
     def hits_of(i):
         at = lax.broadcasted_iota(jnp.int32, (voc, LANES), 0) + fs * voc
-        return at.astype(f32) == small_ref[1:2, span(i)]
+        return at == target_rows[i]
 
     def forward(i):
         y_copy(i).wait_recv()
@@ -245,7 +279,7 @@
         inv = lax.rsqrt(square / (cols * n_fsdp) + eps_norm)
         inv_s[span(i)] = inv
         for j in range(n_fsdp):
-            nm[j] = (hs[j, span(i)].astype(f32) * inv * gain_in[j, 0:1, :cols]).astype(bf)
+            nm[j] = (hs[j, span(i)].astype(f32) * inv * gain_in[j]).astype(bf)
         lg[i] = jnp.zeros((voc, LANES), f32)
 
         @pl.loop(0, n_fsdp)
@@ -262,6 +296,10 @@
         st_out[i, 3:8] = jnp.zeros((5, LANES), f32)
         for j in range(1, n_fsdp):
             t_copy(j, i).start()
+
+        @pl.when(i + 2 < nch)
+        def _():
+            y_copy(i + 2).start()
 
     def backward(i):
         for j in range(1, n_fsdp):
@@ -276,8 +314,8 @@
             total += s[1:2] * jnp.exp(s[0:1] - top)
             chosen += s[2:3]
         lse = top + jnp.log(total)
-        adv, mask = rowv[0:1, span(i)], rowv[1:2, span(i)]
-        ratio = jnp.exp(chosen - lse - small_ref[2:3, span(i)])
+        adv, mask = adv_rows[i], mask_rows[i]
+        ratio = jnp.exp(chosen - lse - old_rows[i])
         first = ratio * adv
         second = jnp.clip(ratio, clip_low, clip_high) * adv
         policy = -jnp.minimum(first, second)
@@ -303,7 +341,16 @@
         acc[span(i)] = dn(2)
         c_copy(1, i).wait_recv()
         y_out[span(i)] = (acc[span(i)] + c_in[1, span(i)].astype(f32)).astype(bf)
-        r_copy(i).start()
+
+        @pl.when(i == nch - 2)
+        def _():
+            for n in range(nch - 1):
+                r_copy(n).start()
+
+        @pl.when(i == nch - 1)
+        def _():
+            r_copy(i).start()
+
         acc[span(i)] = dn(0)
         c_copy(0, i).wait_recv()
         acc[span(i)] += c_in[0, span(i)].astype(f32)
@@ -324,8 +371,8 @@
         acc[span(i)] = grad
         h = hs[0, span(i)].astype(f32)
         prod = grad * h
-        g_out[:, :cols] += jnp.sum((prod * inv_s[span(i)]).reshape(LANES // 8, 8, cols), axis=0)
-        part = jnp.sum(prod * gain_in[0, 0:1, :cols], axis=1, keepdims=True)
+        gsum[...] += jnp.sum((prod * inv_s[span(i)]).reshape(LANES // 8, 8, cols), axis=0)
+        part = jnp.sum(prod * gain_in[0], axis=1, keepdims=True)
         d_out[i] = jnp.transpose(jnp.broadcast_to(part, (LANES, LANES)))[:8]
         for j in range(1, n_fsdp):
             d_copy(j, i).start()
@@ -339,7 +386,7 @@
         inv = inv_s[span(i)]
         scale = inv * inv * inv * column / (cols * n_fsdp)
         gh_ref[span(i)] = (
-            inv * (acc[span(i)] * gain_in[0, 0:1, :cols])
+            inv * (acc[span(i)] * gain_in[0])
             - hs[0, span(i)].astype(f32) * scale
         ).astype(bf)
 
@@ -359,20 +406,30 @@
     @pl.loop(0, nch)
     def _(p):
         x_out[0, span(p)] = dw(p, 1 - zh, 1 - x).astype(bf)
-        x_copy(0, p).start()
+        x_copy(0, 2 * p).start()
+        x_copy(0, 2 * p + 1).start()
 
     @pl.loop(0, nch)
     def _(p):
         x_out[1, span(p)] = dw(p, zh, 1 - x).astype(bf)
-        x_copy(1, p).start()
+        x_copy(1, 2 * p).start()
+        x_copy(1, 2 * p + 1).start()
+        fin[span(p)] = dw(p, 1 - zh, x)
+
+        @pl.loop(2 * p, 2 * p + 2)
+        def _(q):
+            x_copy(0, q).wait_recv()
+            z_out[piece(q)] = (fin[piece(q)] + x_in[0, piece(q)].astype(f32)).astype(bf)
+            h_copy(q).start()
+
         dots(p)
-        fin[span(p)] = dw(p, 1 - zh, x)
-        x_copy(0, p).wait_recv()
-        z_out[span(p)] = (fin[span(p)] + x_in[0, span(p)].astype(f32)).astype(bf)
-        h_copy(p).start()
-        finish(p)
-
-    g_out[:, cols:] = loss_s[...]
+
+    nb = cols // LANES
+    column_sums = jnp.sum(gsum[...], axis=0, keepdims=True)
+    g_out[...] = jnp.zeros_like(g_out)
+    for b in range(nb):
+        g_out[b : b + 1] = column_sums[:, b * LANES : (b + 1) * LANES]
+    g_out[nb : nb + 1] = loss_s[0:1]
 
     @pl.loop(1, n_dp)
     def _(k):
@@ -381,8 +438,19 @@
     @pl.loop(0, nch)
     def _(p):
         fin[span(p)] = dw(p, zh, x)
-        x_copy(1, p).wait_recv()
+        finish(p)
+
+    @pl.loop(0, nch)
+    def _(p):
+        x_copy(1, 2 * p).wait_recv()
+        x_copy(1, 2 * p + 1).wait_recv()
         fin[span(p)] += x_in[1, span(p)].astype(f32)
+
+    mine = gain_in[fs ^ (2 * zh + zl), :, pl.ds(pl.multiple_of(x * feats, LANES), feats)]
+    for p in range(nch):
+        h_copy(2 * p).wait_recv()
+        h_copy(2 * p + 1).wait_recv()
+        gw_ref[:, span(p)] = jnp.transpose((fin[span(p)] + z_in[span(p)].astype(f32)) * mine)
 
     gg_ref[...] = g_out[...]
 
@@ -391,16 +459,7 @@
         g_copy(k).wait_recv()
         gg_ref[...] += g_in[k]
 
-    gg_ref[:, cols:] = jnp.broadcast_to(
-        jnp.sum(gg_ref[0:1, cols:], axis=1, keepdims=True) / cnt[0:1], (8, LANES)
-    )
-    gg_ref[0:1, :cols] = jnp.sum(gg_ref[:, :cols], axis=0, keepdims=True)
-
-    mine = gain_in[fs ^ (2 * zh + zl), 0:1, pl.ds(pl.multiple_of(x * feats, LANES), feats)]
-    for p in range(nch):
-        h_copy(p).wait_recv()
-        piece = (fin[span(p)] + z_in[span(p)].astype(f32)) * mine
-        gw_ref[:, span(p)] = jnp.transpose(piece)
+    gg_ref[nb : nb + 1] = jnp.sum(gg_ref[nb : nb + 1], axis=1, keepdims=True) / cnt[0:1]
 
     @pl.loop(0, nch)
     def _(i):
@@ -409,12 +468,14 @@
         f_copy(i).wait_send()
         l_copy(i).wait_send()
         r_copy(i).wait_send()
-        h_copy(i).wait_send()
+        for q in range(2):
+            h_copy(2 * i + q).wait_send()
+            x_copy(0, 2 * i + q).wait_send()
+            x_copy(1, 2 * i + q).wait_send()
         for k in range(2):
             z_copy(k, i).wait_send()
             w_copy(k, i).wait_send()
             c_copy(k, i).wait_send()
-            x_copy(k, i).wait_send()
         for j in range(1, n_fsdp):
             t_copy(j, i).wait_send()
             d_copy(j, i).wait_send()
@@ -428,13 +489,46 @@
         g_copy(k).wait_send()
 
 
-def whole(small, hidden, head, length_max):
+def write_kernel(gh_ref, gw_ref, gg_ref, loss_out, gh_out, gg_out, gw_out, sems):
+    copies = [
+        pltpu.make_async_copy(gh_ref, gh_out, sems.at[0]),
+        pltpu.make_async_copy(gw_ref, gw_out, sems.at[1]),
+    ]
+    for copy in copies:
+        copy.start()
+    nb = gg_out.shape[0]
+    gg_out[...] = gg_ref[:nb]
+    loss_out[...] = gg_ref[nb : nb + 1, :1]
+    for copy in copies:
+        copy.wait()
+
+
+def write(gh, gw, gg, nb):
+    vm = pl.BlockSpec(memory_space=pltpu.VMEM)
+    anywhere = pl.BlockSpec(memory_space=pl.ANY)
+    return pl.pallas_call(
+        write_kernel,
+        out_shape=(
+            jax.ShapeDtypeStruct((1, 1), jnp.float32),
+            jax.ShapeDtypeStruct(gh.shape, gh.dtype),
+            jax.ShapeDtypeStruct((nb, LANES), jnp.float32),
+            jax.ShapeDtypeStruct(gw.shape, gw.dtype),
+        ),
+        in_specs=[vm, vm, vm],
+        out_specs=(vm, anywhere, vm, anywhere),
+        scratch_shapes=[pltpu.SemaphoreType.DMA((2,))],
+        compiler_params=pltpu.CompilerParams(vmem_limit_bytes=8 * 1024 * 1024),
+    )(gh, gw, gg)
+
+
+def whole(gain_row, targets, old_logp, lengths, rewards, group_slot, hidden, head):
     n_dp, n_fsdp = lax.axis_size("dp"), lax.axis_size("fsdp")
+    resp_here, length_max = targets.shape
     rows, cols = hidden.shape
     voc, width = head.shape
     feats = width // n_dp
     nch = rows // LANES
-    wide = cols + LANES
+    tall = (cols // LANES + 8) // 8 * 8
     bf, f32 = jnp.bfloat16, jnp.float32
     vm = pl.BlockSpec(memory_space=pltpu.VMEM)
     anywhere = pl.BlockSpec(memory_space=pl.ANY)
@@ -442,23 +536,31 @@
     return pl.pallas_call(
         functools.partial(whole_kernel, n_dp, n_fsdp, length_max),
         out_shape=(
-            jax.ShapeDtypeStruct((rows, cols), bf),
-            jax.ShapeDtypeStruct((feats, voc), f32),
-            jax.ShapeDtypeStruct((8, wide), f32),
+            pltpu.VMEM((rows, cols), bf),
+            pltpu.VMEM((feats, voc), f32),
+            pltpu.VMEM((tall, LANES), f32),
         ),
-        in_specs=[vm, anywhere, anywhere],
+        in_specs=[vm] + [anywhere] * 7,
         out_specs=(vm, vm, vm),
         scratch_shapes=[
+            pltpu.VMEM((resp_here, length_max), jnp.int32),
+            pltpu.VMEM((resp_here, length_max), f32),
+            pltpu.SMEM((resp_here,), jnp.int32),
+            pltpu.SMEM((resp_here,), f32),
+            pltpu.SMEM((resp_here,), jnp.int32),
+            pltpu.VMEM((nch, 1, LANES), jnp.int32),
+            pltpu.VMEM((nch, 1, LANES), f32),
+            pltpu.VMEM((nch, 1, LANES), f32),
+            pltpu.VMEM((nch, 1, LANES), f32),
             pltpu.VMEM((voc, width), bf),
             pltpu.VMEM((n_fsdp, rows, cols), bf),
             pltpu.VMEM((2, rows, cols), bf),
             pltpu.VMEM((n_fsdp, LANES, cols), bf),
             pltpu.VMEM((nch, voc, LANES), f32),
             pltpu.VMEM((rows, 1), f32),
-            pltpu.VMEM((8, rows), f32),
             pltpu.VMEM((8, LANES), f32),
             pltpu.VMEM((8, LANES), f32),
-            pltpu.VMEM((n_fsdp, *small.shape), f32),
+            pltpu.VMEM((n_fsdp, 1, cols), f32),
             pltpu.VMEM((8, LANES), f32),
             pltpu.VMEM((n_dp, 8, LANES), f32),
             pltpu.VMEM((nch, 8, LANES), f32),
@@ -477,10 +579,12 @@
             pltpu.VMEM((voc, feats), bf),
             pltpu.VMEM((voc, feats), bf),
             pltpu.VMEM((voc, feats), f32),
-            pltpu.VMEM((8, wide), f32),
-            pltpu.VMEM((n_dp, 8, wide), f32),
+            pltpu.VMEM((8, cols), f32),
+            pltpu.VMEM((tall, LANES), f32),
+            pltpu.VMEM((n_dp, tall, LANES), f32),
             dma((nch,)),
             dma((1,)),
+            dma((5,)),
             dma((2, nch)),
             dma((2, nch)),
             dma((2, nch)),
@@ -493,14 +597,14 @@
             dma((2, 2, nch)),
             dma((2, nch)),
             dma((2, n_fsdp, nch)),
-            dma((2, 2, nch)),
-            dma((2, nch)),
+            dma((2, 2, 2 * nch)),
+            dma((2, 2 * nch)),
             dma((2, n_dp)),
         ],
         compiler_params=pltpu.CompilerParams(
             collective_id=1, has_side_effects=True, vmem_limit_bytes=60 * 1024 * 1024
         ),
-    )(small, hidden, head)
+    )(gain_row, targets, old_logp, lengths, rewards, group_slot, hidden, head)
 
 
 def fits(hidden, head):
@@ -513,7 +617,7 @@
         and (width // n_dp) % LANES == 0
         and rows % LANES == 0
         and rows == voc
-        and rows <= hidden.shape[2]
+        and hidden.shape[1] % LANES == 0
     )
 
 
@@ -521,31 +625,23 @@
     if not fits(hidden, head):
         return general(hidden, gain, head, targets, lengths, old_logp, rewards, group_slot)
     resp_here, length_max, cols = hidden.shape
-    rows = resp_here * length_max
-
-    def row(values):
-        flat = values.astype(jnp.float32).reshape(-1)
-        return jnp.pad(flat, (0, cols - flat.shape[0]))
-
-    def per_position(values):
-        return row(jnp.broadcast_to(values[:, None], (resp_here, length_max)))
-
-    small = jnp.stack(
-        [
-            row(gain),
-            row(targets),
-            row(old_logp),
-            per_position(lengths),
-            per_position(rewards),
-            per_position(group_slot // GROUP),
-            jnp.zeros((cols,), jnp.float32),
-            jnp.zeros((cols,), jnp.float32),
-        ]
-    )
-    grad_h, grad_head_t, sums = whole(small, hidden.reshape(rows, cols), head, length_max)
-    loss = sums[0, cols]
-    grad_gain = sums[0, :cols]
-    return (loss, grad_h.reshape(resp_here, length_max, cols), grad_gain, grad_head_t)
+    grad_h, grad_head_t, sums = whole(
+        gain.astype(jnp.float32)[None, :],
+        targets,
+        old_logp,
+        lengths,
+        rewards,
+        group_slot,
+        hidden.reshape(resp_here * length_max, cols),
+        head,
+    )
+    loss, grad_h, grad_gain, grad_head_t = write(grad_h, grad_head_t, sums, cols // LANES)
+    return (
+        loss.reshape(()),
+        grad_h.reshape(resp_here, length_max, cols),
+        grad_gain.reshape(cols),
+        grad_head_t,
+    )
 
 
 def tail_kernel(

time: 127 us -> 91 us (0.72)
  Pallas kernels: 116 us -> 88.9 us
  local copies, waits for them, and re-layouts: 8.57 us -> 1.28 us
  other arithmetic: 2.01 us -> 0 us
    pallas_call x1, Pallas kernels: 116 us -> 86.7 us  [whole(): pl.pallas_call(functools.partial(whole_kernel, n_dp, n_fsdp, length_max),...]
    unnamed x14 -> x0, local copies, waits for them, and re-layouts: 4.55 us -> none
    slice x2 -> x0, local copies, waits for them, and re-layouts: 2.58 us -> none  [the longest x1 1.4 us: body(): grad_gain = sums[0, :cols]]
    pallas_call x0 -> x1, Pallas kernels: none -> 2.11 us  [write(): pl.pallas_call(write_kernel, out_shape=(jax.ShapeDtypeStruct((1, 1), jnp....]
    another operation x8 -> x0, local copies, waits for them, and re-layouts: 1.41 us -> none  [body(): jnp.stack([row(gain), row(targets), row(old_logp), per_position(lengths),...]
    convert_element_type x2 -> x0, other arithmetic: 1.33 us -> none  [row(): flat = values.astype(jnp.float32).reshape(-1)]
    broadcast_in_dim x0 -> x1, local copies, waits for them, and re-layouts: none -> 1.28 us  [body(): gain.astype(jnp.float32)[None, :]]
where the time goes in v2:
time: 91 us; the launch traced here: 90.8 us
  Pallas kernels  88.9 us (98%)
  local copies, waits for them, and re-layouts  1.28 us (1%)
    pallas_call x1, Pallas kernels, whole(): pl.pallas_call(functools.partial(whole_kernel, n_dp, n_fsdp, length_max),...  86.7 us
    pallas_call x1, Pallas kernels, write(): pl.pallas_call(write_kernel, out_shape=(jax.ShapeDtypeStruct((1, 1), jnp....  2.11 us

profile of v2, /device:TPU:0, one launch (start us, length us, event | category | flops | bytes accessed | tf_op | source)
XLA Modules:
  0.0 90.8 jit_solution(767231176834678674)
XLA Ops:
  0.6 1.3 %reshape.24.gain_ref = f32[1,1280]{1,0:T(1,128)} reshape(bf16[1280]{0:T(1024)(128)(2,1)} %param.9) | data formatting | bytes 7680 | tf_op jit(solution)/shard_map/broadcast_in_dim | solution.py:629
  1.9 86.7 %shard_map.111 = (bf16[512,1280]{1,0:T(8,128)(2,1)S(1)}, f32[640,512]{1,0:T(8,128)S(1)}, f32[16,128]{1,0:T(8,128)S(1)}) custom-call(f32[1,1280]{1,0:T(1,128)} %reshape.24.gain_ref, s32[2,256]{1,0:T(2,128)} %targets_hbm.1, f32[2,256]{1,0:T(2,128)} %old_hbm.1, s32[2]{0:T(128)} %lengths_hbm.1, f32[2]{0:T(128)} %rewards_hbm.1, s32[2]{0:T(128)} %slots_hbm.1, ...), custom_call_target="tpu_custom_call" | custom-call | tf_op jit(solution)/shard_map/pallas_call | solution.py:536
  88.7 2.1 %shard_map.112 = (f32[1,1]{1,0:T(1,128)}, bf16[512,1280]{1,0:T(8,128)(2,1)}, f32[10,128]{1,0:T(8,128)}, f32[640,512]{1,0:T(8,128)}) custom-call(bf16[512,1280]{1,0:T(8,128)(2,1)S(1)} %get-tuple-element.11.gh_ref, f32[640,512]{1,0:T(8,128)S(1)} %get-tuple-element.12.gw_ref, f32[16,128]{1,0:T(8,128)S(1)} %get-tuple-element.13.gg_ref), custom_call_target="tpu_custom_call" | custom-call | tf_op jit(solution)/shard_map/pallas_call | solution.py:509

commit v3 on v2

--- a/solution.py
+++ b/solution.py
@@ -23,7 +23,7 @@
     n_dp,
     n_fsdp,
     length_max,
-    gain_ref,
+    gain_hbm,
     targets_hbm,
     old_hbm,
     lengths_hbm,
@@ -39,16 +39,22 @@
     lengths,
     rewards,
     slots,
+    gain_flat,
+    gain_row,
     target_rows,
     old_rows,
     adv_rows,
     mask_rows,
     head,
+    turned,
+    sums,
     hs,
     hz,
     nm,
     lg,
     inv_s,
+    inv_rows,
+    squares,
     cnt,
     loss_s,
     gain_in,
@@ -63,6 +69,8 @@
     y_out,
     y_in,
     acc,
+    mid,
+    left,
     d_out,
     d_in,
     x_out,
@@ -76,6 +84,7 @@
     own_sem,
     head_sem,
     small_sem,
+    sent,
     ysem,
     nsem,
     fsem,
@@ -89,6 +98,7 @@
     rsem,
     dsem,
     xsem,
+    vsem,
     hsem,
     gsem,
 ):
@@ -99,28 +109,27 @@
     rows, cols = hidden_ref.shape
     voc = head_hbm.shape[0]
     nch = rows // LANES
-    half = LANES // 2
+    quarter = LANES // 4
     feats = gw_ref.shape[0]
     resp_here = rows // length_max
     groups_all = resp_here * n_dp // GROUP
     f32, bf = jnp.float32, jnp.bfloat16
-    pick = (c + 1 - zl) % 2
 
     def span(i):
         return pl.ds(pl.multiple_of(i * LANES, LANES), LANES)
 
     def piece(p):
-        return pl.ds(pl.multiple_of(p * half, half), half)
+        return pl.ds(pl.multiple_of(p * quarter, quarter), quarter)
 
     def shard(j):
         return pl.ds(pl.multiple_of((fs ^ j) * cols, LANES), cols)
 
-    def remote(src, dst, sems, at, to):
+    def remote(src, dst, kind, arrival, to):
         return pltpu.make_async_remote_copy(
             src_ref=src,
             dst_ref=dst,
-            send_sem=sems.at[(0, *at)],
-            recv_sem=sems.at[(1, *at)],
+            send_sem=sent.at[kind],
+            recv_sem=arrival,
             device_id=to,
             device_id_type=MESH,
         )
@@ -133,52 +142,64 @@
 
     head_copy = pltpu.make_async_copy(head_hbm, head, head_sem.at[0])
 
-    def y_copy(i):
-        return remote(hs.at[0, span(i)], hs.at[2, span(i)], ysem, (i,), across)
+    def y_copy(i, b):
+        size = LANES * 3 // 8 if b else LANES * 5 // 8
+        at = pl.ds(pl.multiple_of(i * LANES + b * (LANES - size), 16), size)
+        return remote(hs.at[0, at], hs.at[2, at], 0, ysem.at[i], across)
 
     def n_copy(i):
-        return remote(hs.at[0, span(i)], hs.at[1, span(i)], nsem, (i,), core)
+        return remote(hs.at[0, span(i)], hs.at[1, span(i)], 1, nsem.at[i], core)
 
     def f_copy(i):
-        return remote(hs.at[2, span(i)], hs.at[3, span(i)], fsem, (i,), core)
+        return remote(hs.at[2, span(i)], hs.at[3, span(i)], 2, fsem.at[i], core)
 
     def z_copy(k, i):
-        part = pl.ds(pl.multiple_of(i * LANES + c * half, half), half)
-        return remote(hs.at[2 * k + pick, part], hz.at[k, part], zsem, (k, i), near)
+        return remote(hs.at[2 * k, span(i)], hz.at[k, span(i)], 3, zsem.at[k, i], near)
 
     def w_copy(k, i):
-        part = pl.ds(pl.multiple_of(i * LANES + c * half, half), half)
-        return remote(hz.at[k, part], hz.at[k, part], wsem, (k, i), core)
+        return remote(hz.at[k, span(i)], hz.at[k, span(i)], 4, wsem.at[0], core)
 
     def s_copy(j):
-        return remote(gain_ref, gain_in.at[j], ssem, (j,), (dp, fs ^ j))
+        return remote(gain_row, gain_in.at[j], 5, ssem.at[0], (dp, fs ^ j))
 
     def m_copy(k):
-        return remote(meta_out, meta_in.at[k], msem, (k,), (dp ^ k, fs))
+        return remote(meta_out, meta_in.at[k], 6, msem.at[0], (dp ^ k, fs))
 
     def t_copy(j, i):
-        return remote(st_out.at[i], st_in.at[j, i], tsem, (j, i), (dp, fs ^ j))
-
-    def l_copy(i):
-        return remote(dls.at[i], dlz.at[i], lsem, (i,), near)
+        return remote(st_out.at[i], st_in.at[j, i], 7, tsem.at[i], (dp, fs ^ j))
+
+    def l_copy(i, p):
+        return remote(dls.at[i, span(p)], dlz.at[i, span(p)], 8, lsem.at[p], near)
 
     def c_copy(k, i):
-        return remote(c_out.at[k, span(i)], c_in.at[k, span(i)], csem, (k, i), core)
+        return remote(c_out.at[k, span(i)], c_in.at[k, span(i)], 9, csem.at[k, i], core)
 
     def r_copy(i):
-        return remote(y_out.at[span(i)], y_in.at[span(i)], rsem, (i,), across)
+        return remote(y_out.at[span(i)], y_in.at[span(i)], 10, rsem.at[i], across)
 
     def d_copy(j, i):
-        return remote(d_out.at[i], d_in.at[j, i], dsem, (j, i), (dp, fs ^ j))
-
-    def x_copy(k, p):
-        return remote(x_out.at[k, piece(p)], x_in.at[k, piece(p)], xsem, (k, p), side)
-
-    def h_copy(p):
-        return remote(z_out.at[piece(p)], z_in.at[piece(p)], hsem, (p,), far)
+        return remote(d_out.at[i], d_in.at[j, i], 11, dsem.at[i], (dp, fs ^ j))
+
+    def x_copy(q):
+        return remote(x_out.at[0, piece(q)], x_in.at[0, piece(q)], 12, xsem.at[q], side)
+
+    def v_copy(p):
+        return remote(x_out.at[1, span(p)], x_in.at[1, span(p)], 13, vsem.at[p], side)
+
+    def h_copy(p, q):
+        at = piece(4 * p + q)
+        return remote(z_out.at[at], z_in.at[at], 14, hsem.at[p], far)
 
     def g_copy(k):
-        return remote(g_out, g_in.at[k], gsem, (k,), (dp ^ k, fs))
+        return remote(g_out, g_in.at[k], 15, gsem.at[0], (dp ^ k, fs))
+
+    def arrived(ref, arrival):
+        remote(ref, ref, 0, arrival, core).wait_recv()
+
+    def drained(ref, kind):
+        remote(ref, ref, kind, ysem.at[0], core).wait_send()
+
+    gives, takes = c != zl, c == zl
 
     barrier = pltpu.get_barrier_semaphore()
     for k in range(1, n_dp):
@@ -197,11 +218,35 @@
             ]
         )
     ]
+    gain_copy = pltpu.make_async_copy(gain_hbm, gain_flat, small_sem.at[5])
+    gain_copy.start()
     for load in loads:
         load.start()
     for i in range(nch):
         own_copy(i).start()
     head_copy.start()
+    pl.semaphore_wait(barrier, n_dp + n_fsdp - 2)
+
+    gain_copy.wait()
+    gain_row[...] = gain_flat[...].astype(f32).reshape(1, cols)
+    for j in range(1, n_fsdp):
+        s_copy(j).start()
+
+    @pl.loop(0, nch)
+    def _(i):
+        own_copy(i).wait()
+
+        @pl.when(i == 0)
+        def _():
+            y_copy(i, 0).start()
+            y_copy(i, 1).start()
+
+        @pl.when(i == 1)
+        def _():
+            y_copy(i, 0).start()
+
+        n_copy(i).start()
+
     for load in loads:
         load.wait()
 
@@ -211,38 +256,32 @@
         tile += jnp.where(lane == slots[r] // GROUP, rewards[r], 0.0)
         tile += jnp.where(lane == groups_all, lengths[r].astype(f32), 0.0)
     meta_out[...] = tile
-
-    pl.semaphore_wait(barrier, n_dp + n_fsdp - 2)
-
-    for j in range(1, n_fsdp):
-        s_copy(j).start()
     for k in range(1, n_dp):
         m_copy(k).start()
 
-    @pl.loop(0, nch)
-    def _(i):
-        own_copy(i).wait()
-        n_copy(i).start()
-
-        @pl.when(i < 2)
-        def _():
-            y_copy(i).start()
+    @pl.when(gives)
+    def _():
+        @pl.loop(0, nch)
+        def _(i):
+            z_copy(0, i).start()
 
     loss_s[...] = jnp.zeros_like(loss_s)
     gsum[...] = jnp.zeros_like(gsum)
     head_copy.wait()
 
+    @pl.loop(0, head.shape[1] // LANES)
+    def _(b):
+        turned[span(b)] = jnp.transpose(head[:, span(b)])
+
     @pl.loop(0, nch)
     def _(i):
         n_copy(i).wait_recv()
-        z_copy(0, i).start()
-
-    gain_in[0] = gain_ref[...]
-    for j in range(1, n_fsdp):
-        s_copy(j).wait_recv()
+
+    gain_in[0] = gain_row[...]
+    arrived(gain_in.at[pl.ds(1, n_fsdp - 1)], ssem.at[0])
+    arrived(meta_in.at[pl.ds(1, n_dp - 1)], msem.at[0])
     total = meta_out[...]
     for k in range(1, n_dp):
-        m_copy(k).wait_recv()
         total += meta_in[k]
 
     def entry(g):
@@ -263,31 +302,35 @@
         at = lax.broadcasted_iota(jnp.int32, (voc, LANES), 0) + fs * voc
         return at == target_rows[i]
 
+    def take(j, i):
+        h = hs[j, span(i)].astype(f32)
+        nm[j] = (h * gain_in[j]).astype(bf)
+        return jnp.sum(h * h, axis=1, keepdims=True)
+
+    def product(j):
+        return jnp.dot(nm[j], turned[shard(j)], preferred_element_type=f32)
+
+    def begin(i):
+        squares[...] = take(0, i) + take(1, i)
+        sums[...] = product(0)
+        sums[...] += product(1)
+
     def forward(i):
-        y_copy(i).wait_recv()
+        arrived(hs.at[2, span(i)], ysem.at[i])
         f_copy(i).start()
-        z_copy(0, i).wait_recv()
-        w_copy(0, i).start()
-        square = jnp.zeros((LANES, 1), f32)
-        for j in range(3):
-            h = hs[j, span(i)].astype(f32)
-            square += jnp.sum(h * h, axis=1, keepdims=True)
+
+        @pl.when(gives)
+        def _():
+            z_copy(1, i).start()
+
+        square = squares[...] + take(2, i)
+        sums[...] += product(2)
         f_copy(i).wait_recv()
-        z_copy(1, i).start()
-        h = hs[3, span(i)].astype(f32)
-        square += jnp.sum(h * h, axis=1, keepdims=True)
+        square += take(3, i)
         inv = lax.rsqrt(square / (cols * n_fsdp) + eps_norm)
         inv_s[span(i)] = inv
-        for j in range(n_fsdp):
-            nm[j] = (hs[j, span(i)].astype(f32) * inv * gain_in[j]).astype(bf)
-        lg[i] = jnp.zeros((voc, LANES), f32)
-
-        @pl.loop(0, n_fsdp)
-        def _(j):
-            lg[i] += lax.dot_general(
-                head[:, shard(j)], nm[j], (((1,), (1,)), ((), ())), preferred_element_type=f32
-            )
-
+        inv_rows[i] = jnp.transpose(jnp.broadcast_to(inv, (LANES, LANES)))[:1]
+        lg[i] = jnp.transpose((sums[...] + product(3)) * inv)
         logits = lg[i]
         top = jnp.max(logits, axis=0, keepdims=True)
         st_out[i, 0:1] = top
@@ -297,13 +340,16 @@
         for j in range(1, n_fsdp):
             t_copy(j, i).start()
 
+        @pl.when(i + 1 < nch)
+        def _():
+            y_copy(i + 1, 1).start()
+
         @pl.when(i + 2 < nch)
         def _():
-            y_copy(i + 2).start()
+            y_copy(i + 2, 0).start()
 
     def backward(i):
-        for j in range(1, n_fsdp):
-            t_copy(j, i).wait_recv()
+        arrived(st_in.at[pl.ds(1, n_fsdp - 1), i], tsem.at[i])
         stats = [st_out[i]] + [st_in[j, i] for j in range(1, n_fsdp)]
         top = stats[0][0:1]
         for s in stats[1:]:
@@ -324,46 +370,73 @@
         active = (first <= second) & jnp.logical_not((adv < 0) & (first < dual_bound * adv))
         slope = slots_all / cnt[0:1] * mask * jnp.where(active, -ratio * adv, 0.0)
         grad = slope * (hits_of(i).astype(f32) - jnp.exp(lg[i] - lse))
-        inv_row = jnp.transpose(jnp.broadcast_to(inv_s[span(i)], (LANES, LANES)))[:1]
-        dls[i] = (grad * inv_row).astype(bf)
-        l_copy(i).start()
-        left = jnp.transpose(grad).astype(bf)
-
+        dls[i] = (grad * inv_rows[i]).astype(bf)
+        l_copy(i, 0).start()
+
+        @pl.when(i < nch - 2)
+        def _():
+            for p in range(1, nch):
+                l_copy(i, p).start()
+
+        left[...] = jnp.transpose(grad).astype(bf)
+
+    def spread(i):
         def dn(j):
-            return jnp.dot(left, head[:, shard(j)], preferred_element_type=f32)
+            return jnp.dot(left[...], head[:, shard(j)], preferred_element_type=f32)
 
         c_out[1, span(i)] = dn(3).astype(bf)
         c_copy(1, i).start()
         c_out[0, span(i)] = dn(1).astype(bf)
         c_copy(0, i).start()
-        z_copy(1, i).wait_recv()
-        w_copy(1, i).start()
-        acc[span(i)] = dn(2)
+        acc[span(i)] = dn(0)
+        mid[span(i)] = dn(2)
+
+    def relay(i):
+        @pl.when(takes)
+        def _():
+            for k in range(2):
+                z_copy(k, i).wait_recv()
+                w_copy(k, i).start()
+
+    def combine(i):
         c_copy(1, i).wait_recv()
-        y_out[span(i)] = (acc[span(i)] + c_in[1, span(i)].astype(f32)).astype(bf)
-
-        @pl.when(i == nch - 2)
+        y_out[span(i)] = (mid[span(i)] + c_in[1, span(i)].astype(f32)).astype(bf)
+        c_copy(0, i).wait_recv()
+        acc[span(i)] += c_in[0, span(i)].astype(f32)
+
+    begin(0)
+
+    @pl.loop(0, nch)
+    def _(i):
+        forward(i)
+
+        @pl.when(i + 1 < nch)
         def _():
-            for n in range(nch - 1):
-                r_copy(n).start()
+            begin(i + 1)
+
+        @pl.when(i > 0)
+        def _():
+            relay(i - 1)
+            spread(i - 1)
+
+        @pl.when(i > 1)
+        def _():
+            combine(i - 2)
 
         @pl.when(i == nch - 1)
         def _():
-            r_copy(i).start()
-
-        acc[span(i)] = dn(0)
-        c_copy(0, i).wait_recv()
-        acc[span(i)] += c_in[0, span(i)].astype(f32)
-
-    @pl.loop(0, nch + 1)
-    def _(i):
-        @pl.when(i < nch)
-        def _():
-            forward(i)
-
-        @pl.when(i > 0)
-        def _():
-            backward(i - 1)
+            for n in range(nch - 2):
+                r_copy(n).start()
+
+        backward(i)
+
+    for p in range(1, nch):
+        for i in range(nch - 2, nch):
+            l_copy(i, p).start()
+    relay(nch - 1)
+    spread(nch - 1)
+    combine(nch - 2)
+    r_copy(nch - 2).start()
 
     def dots(i):
         r_copy(i).wait_recv()
@@ -379,8 +452,8 @@
 
     def finish(i):
         whole = d_out[i]
+        arrived(d_in.at[pl.ds(1, n_fsdp - 1), i], dsem.at[i])
         for j in range(1, n_fsdp):
-            d_copy(j, i).wait_recv()
             whole += d_in[j, i]
         column = jnp.transpose(jnp.broadcast_to(whole[:1], (LANES, LANES)))[:, :1]
         inv = inv_s[span(i)]
@@ -392,36 +465,42 @@
 
     def dw(p, zb, xb):
         at = pl.ds(pl.multiple_of(xb * feats, LANES), feats)
-        left = jnp.concatenate([dls[i, span(p)] for i in range(nch)], axis=1)
+        here = jnp.concatenate([dls[i, span(p)] for i in range(nch)], axis=1)
         other = jnp.concatenate([dlz[i, span(p)] for i in range(nch)], axis=1)
         return jnp.dot(
-            left, hs[fs ^ (2 * zb + zl), :, at], preferred_element_type=f32
+            here, hs[fs ^ (2 * zb + zl), :, at], preferred_element_type=f32
         ) + jnp.dot(other, hz[y ^ zb, :, at], preferred_element_type=f32)
 
-    for i in range(nch):
-        l_copy(i).wait_recv()
-        w_copy(0, i).wait_recv()
-        w_copy(1, i).wait_recv()
+    @pl.when(gives)
+    def _():
+        arrived(hz, wsem.at[0])
 
     @pl.loop(0, nch)
     def _(p):
+        arrived(dlz.at[:, span(p)], lsem.at[p])
         x_out[0, span(p)] = dw(p, 1 - zh, 1 - x).astype(bf)
-        x_copy(0, 2 * p).start()
-        x_copy(0, 2 * p + 1).start()
+        for q in range(4):
+            x_copy(4 * p + q).start()
+
+    combine(nch - 1)
+    r_copy(nch - 1).start()
 
     @pl.loop(0, nch)
     def _(p):
         x_out[1, span(p)] = dw(p, zh, 1 - x).astype(bf)
-        x_copy(1, 2 * p).start()
-        x_copy(1, 2 * p + 1).start()
+        v_copy(p).start()
         fin[span(p)] = dw(p, 1 - zh, x)
 
-        @pl.loop(2 * p, 2 * p + 2)
+        @pl.loop(0, 4)
         def _(q):
-            x_copy(0, q).wait_recv()
-            z_out[piece(q)] = (fin[piece(q)] + x_in[0, piece(q)].astype(f32)).astype(bf)
-            h_copy(q).start()
-
+            at = piece(4 * p + q)
+            x_copy(4 * p + q).wait_recv()
+            z_out[at] = (fin[at] + x_in[0, at].astype(f32)).astype(bf)
+            h_copy(p, q).start()
+
+    @pl.loop(0, nch)
+    def _(p):
+        fin[span(p)] = dw(p, zh, x)
         dots(p)
 
     nb = cols // LANES
@@ -431,68 +510,66 @@
         g_out[b : b + 1] = column_sums[:, b * LANES : (b + 1) * LANES]
     g_out[nb : nb + 1] = loss_s[0:1]
 
-    @pl.loop(1, n_dp)
-    def _(k):
+    for k in range(1, n_dp):
         g_copy(k).start()
 
     @pl.loop(0, nch)
     def _(p):
-        fin[span(p)] = dw(p, zh, x)
         finish(p)
 
     @pl.loop(0, nch)
     def _(p):
-        x_copy(1, 2 * p).wait_recv()
-        x_copy(1, 2 * p + 1).wait_recv()
+        v_copy(p).wait_recv()
         fin[span(p)] += x_in[1, span(p)].astype(f32)
 
     mine = gain_in[fs ^ (2 * zh + zl), :, pl.ds(pl.multiple_of(x * feats, LANES), feats)]
     for p in range(nch):
-        h_copy(2 * p).wait_recv()
-        h_copy(2 * p + 1).wait_recv()
+        arrived(z_in.at[span(p)], hsem.at[p])
         gw_ref[:, span(p)] = jnp.transpose((fin[span(p)] + z_in[span(p)].astype(f32)) * mine)
 
-    gg_ref[...] = g_out[...]
-
-    @pl.loop(1, n_dp)
-    def _(k):
-        g_copy(k).wait_recv()
-        gg_ref[...] += g_in[k]
-
+    arrived(g_in.at[pl.ds(1, n_dp - 1)], gsem.at[0])
+    whole = g_out[...]
+    for k in range(1, n_dp):
+        whole += g_in[k]
+    gg_ref[...] = whole
     gg_ref[nb : nb + 1] = jnp.sum(gg_ref[nb : nb + 1], axis=1, keepdims=True) / cnt[0:1]
 
-    @pl.loop(0, nch)
-    def _(i):
-        y_copy(i).wait_send()
-        n_copy(i).wait_send()
-        f_copy(i).wait_send()
-        l_copy(i).wait_send()
-        r_copy(i).wait_send()
-        for q in range(2):
-            h_copy(2 * i + q).wait_send()
-            x_copy(0, 2 * i + q).wait_send()
-            x_copy(1, 2 * i + q).wait_send()
-        for k in range(2):
-            z_copy(k, i).wait_send()
-            w_copy(k, i).wait_send()
-            c_copy(k, i).wait_send()
-        for j in range(1, n_fsdp):
-            t_copy(j, i).wait_send()
-            d_copy(j, i).wait_send()
-
-    for j in range(1, n_fsdp):
-        s_copy(j).wait_send()
-
-    @pl.loop(1, n_dp)
-    def _(k):
-        m_copy(k).wait_send()
-        g_copy(k).wait_send()
+    drained(hs.at[0], 0)
+    drained(hs.at[0], 1)
+    drained(hs.at[2], 2)
+
+    @pl.when(gives)
+    def _():
+        drained(hz, 3)
+
+    @pl.when(takes)
+    def _():
+        drained(hz, 4)
+
+    drained(gain_in.at[pl.ds(1, n_fsdp - 1)], 5)
+    drained(meta_in.at[pl.ds(1, n_dp - 1)], 6)
+    drained(st_in.at[pl.ds(1, n_fsdp - 1)], 7)
+    drained(dls, 8)
+    drained(c_out, 9)
+    drained(y_out, 10)
+    drained(d_in.at[pl.ds(1, n_fsdp - 1)], 11)
+    drained(x_out.at[0], 12)
+    drained(x_out.at[1], 13)
+    drained(z_out, 14)
+    drained(g_in.at[pl.ds(1, n_dp - 1)], 15)
 
 
 def write_kernel(gh_ref, gw_ref, gg_ref, loss_out, gh_out, gg_out, gw_out, sems):
+    parts = sems.shape[1]
+
+    def part(ref, n):
+        size = ref.shape[0] // parts
+        return ref.at[pl.ds(n * size, size)]
+
     copies = [
-        pltpu.make_async_copy(gh_ref, gh_out, sems.at[0]),
-        pltpu.make_async_copy(gw_ref, gw_out, sems.at[1]),
+        pltpu.make_async_copy(part(src, n), part(dst, n), sems.at[m, n])
+        for m, (src, dst) in enumerate([(gw_ref, gw_out), (gh_ref, gh_out)])
+        for n in range(parts)
     ]
     for copy in copies:
         copy.start()
@@ -516,12 +593,12 @@
         ),
         in_specs=[vm, vm, vm],
         out_specs=(vm, anywhere, vm, anywhere),
-        scratch_shapes=[pltpu.SemaphoreType.DMA((2,))],
+        scratch_shapes=[pltpu.SemaphoreType.DMA((2, 4))],
         compiler_params=pltpu.CompilerParams(vmem_limit_bytes=8 * 1024 * 1024),
     )(gh, gw, gg)
 
 
-def whole(gain_row, targets, old_logp, lengths, rewards, group_slot, hidden, head):
+def whole(gain, targets, old_logp, lengths, rewards, group_slot, hidden, head):
     n_dp, n_fsdp = lax.axis_size("dp"), lax.axis_size("fsdp")
     resp_here, length_max = targets.shape
     rows, cols = hidden.shape
@@ -540,7 +617,7 @@
             pltpu.VMEM((feats, voc), f32),
             pltpu.VMEM((tall, LANES), f32),
         ),
-        in_specs=[vm] + [anywhere] * 7,
+        in_specs=[anywhere] * 8,
         out_specs=(vm, vm, vm),
         scratch_shapes=[
             pltpu.VMEM((resp_here, length_max), jnp.int32),
@@ -548,16 +625,22 @@
             pltpu.SMEM((resp_here,), jnp.int32),
             pltpu.SMEM((resp_here,), f32),
             pltpu.SMEM((resp_here,), jnp.int32),
+            pltpu.VMEM((cols,), bf),
+            pltpu.VMEM((1, cols), f32),
             pltpu.VMEM((nch, 1, LANES), jnp.int32),
             pltpu.VMEM((nch, 1, LANES), f32),
             pltpu.VMEM((nch, 1, LANES), f32),
             pltpu.VMEM((nch, 1, LANES), f32),
             pltpu.VMEM((voc, width), bf),
+            pltpu.VMEM((width, voc), bf),
+            pltpu.VMEM((LANES, voc), f32),
             pltpu.VMEM((n_fsdp, rows, cols), bf),
             pltpu.VMEM((2, rows, cols), bf),
             pltpu.VMEM((n_fsdp, LANES, cols), bf),
             pltpu.VMEM((nch, voc, LANES), f32),
             pltpu.VMEM((rows, 1), f32),
+            pltpu.VMEM((nch, 1, LANES), f32),
+            pltpu.VMEM((LANES, 1), f32),
             pltpu.VMEM((8, LANES), f32),
             pltpu.VMEM((8, LANES), f32),
             pltpu.VMEM((n_fsdp, 1, cols), f32),
@@ -572,6 +655,8 @@
             pltpu.VMEM((rows, cols), bf),
             pltpu.VMEM((rows, cols), bf),
             pltpu.VMEM((rows, cols), f32),
+            pltpu.VMEM((rows, cols), f32),
+            pltpu.VMEM((LANES, voc), bf),
             pltpu.VMEM((nch, 8, LANES), f32),
             pltpu.VMEM((n_fsdp, nch, 8, LANES), f32),
             pltpu.VMEM((2, voc, feats), bf),
@@ -584,27 +669,29 @@
             pltpu.VMEM((n_dp, tall, LANES), f32),
             dma((nch,)),
             dma((1,)),
-            dma((5,)),
+            dma((6,)),
+            dma((16,)),
+            dma((nch,)),
+            dma((nch,)),
+            dma((nch,)),
             dma((2, nch)),
+            dma((1,)),
+            dma((1,)),
+            dma((1,)),
+            dma((nch,)),
+            dma((nch,)),
             dma((2, nch)),
-            dma((2, nch)),
-            dma((2, 2, nch)),
-            dma((2, 2, nch)),
-            dma((2, n_fsdp)),
-            dma((2, n_dp)),
-            dma((2, n_fsdp, nch)),
-            dma((2, nch)),
-            dma((2, 2, nch)),
-            dma((2, nch)),
-            dma((2, n_fsdp, nch)),
-            dma((2, 2, 2 * nch)),
-            dma((2, 2 * nch)),
-            dma((2, n_dp)),
+            dma((nch,)),
+            dma((nch,)),
+            dma((4 * nch,)),
+            dma((nch,)),
+            dma((nch,)),
+            dma((1,)),
         ],
         compiler_params=pltpu.CompilerParams(
             collective_id=1, has_side_effects=True, vmem_limit_bytes=60 * 1024 * 1024
         ),
-    )(gain_row, targets, old_logp, lengths, rewards, group_slot, hidden, head)
+    )(gain, targets, old_logp, lengths, rewards, group_slot, hidden, head)
 
 
 def fits(hidden, head):
@@ -626,7 +713,7 @@
         return general(hidden, gain, head, targets, lengths, old_logp, rewards, group_slot)
     resp_here, length_max, cols = hidden.shape
     grad_h, grad_head_t, sums = whole(
-        gain.astype(jnp.float32)[None, :],
+        gain,
         targets,
         old_logp,
         lengths,

time: 91 us -> 84.3 us (0.926)
  Pallas kernels: 88.9 us -> 83.5 us
  local copies, waits for them, and re-layouts: 1.28 us -> 0 us
    pallas_call x1, Pallas kernels: 86.7 us -> 81.4 us  [whole(): pl.pallas_call(functools.partial(whole_kernel, n_dp, n_fsdp, length_max),...]
    broadcast_in_dim x1 -> x0, local copies, waits for them, and re-layouts: 1.28 us -> none  [body(): gain.astype(jnp.float32)[None, :]]
where the time goes in v3:
time: 84.3 us; the launch traced here: 84.2 us
  Pallas kernels  83.5 us (99%)
    pallas_call x1, Pallas kernels, whole(): pl.pallas_call(functools.partial(whole_kernel, n_dp, n_fsdp, length_max),...  81.4 us
    pallas_call x1, Pallas kernels, write(): pl.pallas_call(write_kernel, out_shape=(jax.ShapeDtypeStruct((1, 1), jnp....  2.15 us

profile of v3, /device:TPU:0, one launch (start us, length us, event | category | flops | bytes accessed | tf_op | source)
XLA Modules:
  0.0 84.2 jit_solution(15410361787133612182)
XLA Ops:
  0.6 81.4 %shard_map.111 = (bf16[512,1280]{1,0:T(8,128)(2,1)S(1)}, f32[640,512]{1,0:T(8,128)S(1)}, f32[16,128]{1,0:T(8,128)S(1)}) custom-call(bf16[1280]{0:T(1024)(128)(2,1)} %gain_hbm.1, s32[2,256]{1,0:T(2,128)} %targets_hbm.1, f32[2,256]{1,0:T(2,128)} %old_hbm.1, s32[2]{0:T(128)} %lengths_hbm.1, f32[2]{0:T(128)} %rewards_hbm.1, s32[2]{0:T(128)} %slots_hbm.1, ...), custom_call_target="tpu_custom_call" | custom-call | tf_op jit(solution)/shard_map/pallas_call | solution.py:613
  82.0 2.2 %shard_map.112 = (f32[1,1]{1,0:T(1,128)}, bf16[512,1280]{1,0:T(8,128)(2,1)}, f32[10,128]{1,0:T(8,128)}, f32[640,512]{1,0:T(8,128)}) custom-call(bf16[512,1280]{1,0:T(8,128)(2,1)S(1)} %get-tuple-element.11.gh_ref, f32[640,512]{1,0:T(8,128)S(1)} %get-tuple-element.12.gw_ref, f32[16,128]{1,0:T(8,128)S(1)} %get-tuple-element.13.gg_ref), custom_call_target="tpu_custom_call" | custom-call | tf_op jit(solution)/shard_map/pallas_call | solution.py:586

commit v4 on v3

--- a/solution.py
+++ b/solution.py
@@ -475,21 +475,20 @@
     def _():
         arrived(hz, wsem.at[0])
 
-    @pl.loop(0, nch)
-    def _(p):
+    def lead(p):
         arrived(dlz.at[:, span(p)], lsem.at[p])
         x_out[0, span(p)] = dw(p, 1 - zh, 1 - x).astype(bf)
         for q in range(4):
             x_copy(4 * p + q).start()
-
-    combine(nch - 1)
-    r_copy(nch - 1).start()
+        fin[span(p)] = dw(p, 1 - zh, x)
+
+    lead(0)
 
     @pl.loop(0, nch)
     def _(p):
-        x_out[1, span(p)] = dw(p, zh, 1 - x).astype(bf)
-        v_copy(p).start()
-        fin[span(p)] = dw(p, 1 - zh, x)
+        @pl.when(p + 1 < nch)
+        def _():
+            lead(p + 1)
 
         @pl.loop(0, 4)
         def _(q):
@@ -497,6 +496,14 @@
             x_copy(4 * p + q).wait_recv()
             z_out[at] = (fin[at] + x_in[0, at].astype(f32)).astype(bf)
             h_copy(p, q).start()
+
+        @pl.when(p == 0)
+        def _():
+            combine(nch - 1)
+            r_copy(nch - 1).start()
+
+        x_out[1, span(p)] = dw(p, zh, 1 - x).astype(bf)
+        v_copy(p).start()
 
     @pl.loop(0, nch)
     def _(p):

time: 84.3 us -> 82.5 us (0.979)
  Pallas kernels: 83.5 us -> 81.7 us
    pallas_call x1, Pallas kernels: 81.4 us -> 79.6 us  [whole(): pl.pallas_call(functools.partial(whole_kernel, n_dp, n_fsdp, length_max),...]
where the time goes in v4:
time: 82.5 us; the launch traced here: 82.4 us
  Pallas kernels  81.7 us (99%)
    pallas_call x1, Pallas kernels, whole(): pl.pallas_call(functools.partial(whole_kernel, n_dp, n_fsdp, length_max),...  79.6 us
    pallas_call x1, Pallas kernels, write(): pl.pallas_call(write_kernel, out_shape=(jax.ShapeDtypeStruct((1, 1), jnp....  2.15 us

profile of v4, /device:TPU:0, one launch (start us, length us, event | category | flops | bytes accessed | tf_op | source)
XLA Modules:
  0.0 82.4 jit_solution(12853478265110935967)
XLA Ops:
  0.6 79.6 %shard_map.111 = (bf16[512,1280]{1,0:T(8,128)(2,1)S(1)}, f32[640,512]{1,0:T(8,128)S(1)}, f32[16,128]{1,0:T(8,128)S(1)}) custom-call(bf16[1280]{0:T(1024)(128)(2,1)} %gain_hbm.1, s32[2,256]{1,0:T(2,128)} %targets_hbm.1, f32[2,256]{1,0:T(2,128)} %old_hbm.1, s32[2]{0:T(128)} %lengths_hbm.1, f32[2]{0:T(128)} %rewards_hbm.1, s32[2]{0:T(128)} %slots_hbm.1, ...), custom_call_target="tpu_custom_call" | custom-call | tf_op jit(solution)/shard_map/pallas_call | solution.py:620
  80.2 2.2 %shard_map.112 = (f32[1,1]{1,0:T(1,128)}, bf16[512,1280]{1,0:T(8,128)(2,1)}, f32[10,128]{1,0:T(8,128)}, f32[640,512]{1,0:T(8,128)}) custom-call(bf16[512,1280]{1,0:T(8,128)(2,1)S(1)} %get-tuple-element.11.gh_ref, f32[640,512]{1,0:T(8,128)S(1)} %get-tuple-element.12.gw_ref, f32[16,128]{1,0:T(8,128)S(1)} %get-tuple-element.13.gg_ref), custom_call_target="tpu_custom_call" | custom-call | tf_op jit(solution)/shard_map/pallas_call | solution.py:593

commit v5 on v4

--- a/solution.py
+++ b/solution.py
@@ -142,16 +142,20 @@
 
     head_copy = pltpu.make_async_copy(head_hbm, head, head_sem.at[0])
 
+    def cut(i, b):
+        size = LANES * 3 // 8 if b else LANES * 5 // 8
+        return pl.ds(pl.multiple_of(i * LANES + b * (LANES - size), 16), size)
+
     def y_copy(i, b):
-        size = LANES * 3 // 8 if b else LANES * 5 // 8
-        at = pl.ds(pl.multiple_of(i * LANES + b * (LANES - size), 16), size)
-        return remote(hs.at[0, at], hs.at[2, at], 0, ysem.at[i], across)
+        at = cut(i, b)
+        return remote(hs.at[0, at], hs.at[2, at], 0, ysem.at[b, i], across)
 
     def n_copy(i):
         return remote(hs.at[0, span(i)], hs.at[1, span(i)], 1, nsem.at[i], core)
 
-    def f_copy(i):
-        return remote(hs.at[2, span(i)], hs.at[3, span(i)], 2, fsem.at[i], core)
+    def f_copy(i, b):
+        at = cut(i, b)
+        return remote(hs.at[2, at], hs.at[3, at], 2, fsem.at[i], core)
 
     def z_copy(k, i):
         return remote(hs.at[2 * k, span(i)], hz.at[k, span(i)], 3, zsem.at[k, i], near)
@@ -174,14 +178,18 @@
     def c_copy(k, i):
         return remote(c_out.at[k, span(i)], c_in.at[k, span(i)], 9, csem.at[k, i], core)
 
-    def r_copy(i):
-        return remote(y_out.at[span(i)], y_in.at[span(i)], 10, rsem.at[i], across)
+    def r_copy(i, b):
+        at = pl.ds(pl.multiple_of(i * LANES + b * 2 * quarter, 2 * quarter), 2 * quarter)
+        return remote(y_out.at[at], y_in.at[at], 10, rsem.at[i], across)
 
     def d_copy(j, i):
         return remote(d_out.at[i], d_in.at[j, i], 11, dsem.at[i], (dp, fs ^ j))
 
     def x_copy(q):
         return remote(x_out.at[0, piece(q)], x_in.at[0, piece(q)], 12, xsem.at[q], side)
+
+    def e_copy():
+        return remote(x_out.at[0, piece(0)], x_in.at[0, piece(0)], 12, xsem.at[0], far)
 
     def v_copy(p):
         return remote(x_out.at[1, span(p)], x_in.at[1, span(p)], 13, vsem.at[p], side)
@@ -197,7 +205,7 @@
         remote(ref, ref, 0, arrival, core).wait_recv()
 
     def drained(ref, kind):
-        remote(ref, ref, kind, ysem.at[0], core).wait_send()
+        remote(ref, ref, kind, wsem.at[0], core).wait_send()
 
     gives, takes = c != zl, c == zl
 
@@ -316,8 +324,9 @@
         sums[...] += product(1)
 
     def forward(i):
-        arrived(hs.at[2, span(i)], ysem.at[i])
-        f_copy(i).start()
+        for b in range(2):
+            y_copy(i, b).wait_recv()
+            f_copy(i, b).start()
 
         @pl.when(gives)
         def _():
@@ -325,7 +334,7 @@
 
         square = squares[...] + take(2, i)
         sums[...] += product(2)
-        f_copy(i).wait_recv()
+        arrived(hs.at[3, span(i)], fsem.at[i])
         square += take(3, i)
         inv = lax.rsqrt(square / (cols * n_fsdp) + eps_norm)
         inv_s[span(i)] = inv
@@ -423,10 +432,16 @@
         def _():
             combine(i - 2)
 
+        @pl.when(i == nch - 2)
+        def _():
+            r_copy(0, 0).start()
+
         @pl.when(i == nch - 1)
         def _():
-            for n in range(nch - 2):
-                r_copy(n).start()
+            r_copy(0, 1).start()
+            for n in range(1, nch - 2):
+                r_copy(n, 0).start()
+                r_copy(n, 1).start()
 
         backward(i)
 
@@ -436,10 +451,11 @@
     relay(nch - 1)
     spread(nch - 1)
     combine(nch - 2)
-    r_copy(nch - 2).start()
+    r_copy(nch - 2, 0).start()
+    r_copy(nch - 2, 1).start()
 
     def dots(i):
-        r_copy(i).wait_recv()
+        arrived(y_in.at[span(i)], rsem.at[i])
         grad = acc[span(i)] + y_in[span(i)].astype(f32)
         acc[span(i)] = grad
         h = hs[0, span(i)].astype(f32)
@@ -475,40 +491,62 @@
     def _():
         arrived(hz, wsem.at[0])
 
-    def lead(p):
+    def lead(p, direct):
         arrived(dlz.at[:, span(p)], lsem.at[p])
         x_out[0, span(p)] = dw(p, 1 - zh, 1 - x).astype(bf)
-        for q in range(4):
+        if direct:
+            e_copy().start()
+        for q in range(direct, 4):
             x_copy(4 * p + q).start()
         fin[span(p)] = dw(p, 1 - zh, x)
-
-    lead(0)
-
-    @pl.loop(0, nch)
-    def _(p):
-        @pl.when(p + 1 < nch)
-        def _():
-            lead(p + 1)
-
-        @pl.loop(0, 4)
+        if direct:
+            z_out[piece(0)] = fin[piece(0)].astype(bf)
+            h_copy(0, 0).start()
+
+    def follow(p, direct):
+        @pl.loop(direct, 4)
         def _(q):
             at = piece(4 * p + q)
             x_copy(4 * p + q).wait_recv()
             z_out[at] = (fin[at] + x_in[0, at].astype(f32)).astype(bf)
-            h_copy(p, q).start()
-
-        @pl.when(p == 0)
-        def _():
-            combine(nch - 1)
-            r_copy(nch - 1).start()
-
+
+            @pl.when((p < nch - 1) | (q < 2))
+            def _():
+                h_copy(p, q).start()
+
+    def back(p):
         x_out[1, span(p)] = dw(p, zh, 1 - x).astype(bf)
         v_copy(p).start()
 
-    @pl.loop(0, nch)
+    lead(0, 1)
+    lead(1, 0)
+    follow(0, 1)
+    combine(nch - 1)
+    r_copy(nch - 1, 0).start()
+    r_copy(nch - 1, 1).start()
+    lead(2, 0)
+    mid[span(0), :feats] = dw(0, zh, 1 - x)
+    e_copy().wait_recv()
+    mid[piece(0), :feats] += x_in[0, piece(0)].astype(f32)
+    x_out[1, span(0)] = mid[span(0), :feats].astype(bf)
+    v_copy(0).start()
+
+    @pl.loop(1, nch)
     def _(p):
-        fin[span(p)] = dw(p, zh, x)
-        dots(p)
+        @pl.when((p > 1) & (p + 1 < nch))
+        def _():
+            lead(p + 1, 0)
+
+        @pl.when(p > 1)
+        def _():
+            back(p - 1)
+
+        dots(p - 1)
+        follow(p, 0)
+
+    back(nch - 1)
+
+    dots(nch - 1)
 
     nb = cols // LANES
     column_sums = jnp.sum(gsum[...], axis=0, keepdims=True)
@@ -519,6 +557,13 @@
 
     for k in range(1, n_dp):
         g_copy(k).start()
+    for q in range(2, 4):
+        h_copy(nch - 1, q).start()
+
+    @pl.loop(0, nch)
+    def _(p):
+        fin[span(p)] = dw(p, zh, x)
+
 
     @pl.loop(0, nch)
     def _(p):
@@ -678,7 +723,7 @@
             dma((1,)),
             dma((6,)),
             dma((16,)),
-            dma((nch,)),
+            dma((2, nch)),
             dma((nch,)),
             dma((nch,)),
             dma((2, nch)),
@@ -711,6 +756,7 @@
         and (width // n_dp) % LANES == 0
         and rows % LANES == 0
         and rows == voc
+        and rows > 2 * LANES
         and hidden.shape[1] % LANES == 0
     )
 

time: 82.5 us -> 82 us (level)
  no operation moved by 1% of the time
where the time goes in v5:
time: 82 us; the launch traced here: 81.8 us
  Pallas kernels  81.2 us (99%)
    pallas_call x1, Pallas kernels, whole(): pl.pallas_call(functools.partial(whole_kernel, n_dp, n_fsdp, length_max),...  79 us
    pallas_call x1, Pallas kernels, write(): pl.pallas_call(write_kernel, out_shape=(jax.ShapeDtypeStruct((1, 1), jnp....  2.15 us

profile of v5, /device:TPU:0, one launch (start us, length us, event | category | flops | bytes accessed | tf_op | source)
XLA Modules:
  0.0 81.8 jit_solution(9186892603955107106)
XLA Ops:
  0.6 79.0 %shard_map.111 = (bf16[512,1280]{1,0:T(8,128)(2,1)S(1)}, f32[640,512]{1,0:T(8,128)S(1)}, f32[16,128]{1,0:T(8,128)S(1)}) custom-call(bf16[1280]{0:T(1024)(128)(2,1)} %gain_hbm.1, s32[2,256]{1,0:T(2,128)} %targets_hbm.1, f32[2,256]{1,0:T(2,128)} %old_hbm.1, s32[2]{0:T(128)} %lengths_hbm.1, f32[2]{0:T(128)} %rewards_hbm.1, s32[2]{0:T(128)} %slots_hbm.1, ...), custom_call_target="tpu_custom_call" | custom-call | tf_op jit(solution)/shard_map/pallas_call | solution.py:665
  79.7 2.2 %shard_map.112 = (f32[1,1]{1,0:T(1,128)}, bf16[512,1280]{1,0:T(8,128)(2,1)}, f32[10,128]{1,0:T(8,128)}, f32[640,512]{1,0:T(8,128)}) custom-call(bf16[512,1280]{1,0:T(8,128)(2,1)S(1)} %get-tuple-element.11.gh_ref, f32[640,512]{1,0:T(8,128)S(1)} %get-tuple-element.12.gw_ref, f32[16,128]{1,0:T(8,128)S(1)} %get-tuple-element.13.gg_ref), custom_call_target="tpu_custom_call" | custom-call | tf_op jit(solution)/shard_map/pallas_call | solution.py:638
